TPU v7x, 128 devices: a whole 4x4x4 slice. The times are simulated.
128 devices in a mesh: row: 8 (over x, y_lo), col: 16 (over y_hi, z, core).
Axes of the slice: x: 4, y: 4 (y_hi: 2, y_lo: 2; y = y_hi * 2 + y_lo), z: 4, core: 2. Of those that a mesh axis runs over, the one named last changes fastest.
Arguments:
- h_old: float32 [8, 16, 1024, 2048], P('row', 'col'), may hold values from -2 to 2, as said below
- s_old: float32 [8, 16, 1024, 64], P('row', 'col'), may hold values from -100 to 100, as said below
- row_owner: int32 [256], replicated, may hold values from 0 to 15, as said below
- col_owner: int32 [256], replicated, may hold values from 0 to 7, as said below
Outputs:
- h_reduced: float32 [16384, 16384], P('row', 'col')
- panel_factor: float32 [16384, 512], P('row')
Inputs may be any that keep to these rules, and one draw needn't show every extreme that they name: `row_owner`: each aligned run of 16 entries is an ordering of 0 to 15. `col_owner`: each aligned run of 8 entries is an ordering of 0 to 7. `s_old`: the first 512 rows of S_panel form a symmetric positive definite matrix. `h_old`: H is symmetric.
All inputs are finite; a program needn't handle non-finite values.
Results may differ from a plain program's by a relative error of at most 0.00017.
Values sent between devices are 32-bit elements; how exact they have to be, the bound alone decides.
A program may use at most 192 MiB of HBM per device.

v0:
```python
import jax
import jax.numpy as jnp
from jax import lax
from jax.sharding import PartitionSpec as P

ORDER = 16384
PANEL = 512
BLOCK = 64


def split_up(shard, dim, length):
    before, after = (shard.shape[:dim], shard.shape[dim + 1 :])
    return jnp.moveaxis(shard.reshape(*before, length, -1, *after), dim, 0)


def cut_rows(length, count):
    unit = 8 if length >= 8 * count else 1
    return [length // unit * k // count * unit for k in range(1, count)]


def in_order(blocks, dim):
    dims = list(blocks.shape[1:])
    dims[dim] *= blocks.shape[0]
    return jnp.moveaxis(blocks, 0, dim).reshape(dims)


def several_exchanges(shard, axis, pieces, split_dim, concat_dim):
    blocks = split_up(shard, split_dim, lax.axis_size(axis))
    widest = max(range(1, max(2, blocks.ndim - 1)), key=lambda d: blocks.shape[d])
    finished = []
    for share in jnp.split(blocks, cut_rows(blocks.shape[widest], pieces), axis=widest):
        if share.size:
            finished.append(lax.all_to_all(share, axis, split_axis=0, concat_axis=0, tiled=True))
    return in_order(jnp.concatenate(finished, axis=widest), concat_dim)


def sent_together(arrays, axis, split_dim, concat_dim, along):
    ends, at = ([], 0)
    for a in arrays[:-1]:
        at += a.shape[along]
        ends.append(at)
    both = jnp.concatenate(arrays, axis=along)
    return tuple(
        jnp.split(
            lax.all_to_all(both, axis, split_axis=split_dim, concat_axis=concat_dim, tiled=True),
            ends,
            axis=along,
        )
    )


def broadcast(block, axis, holder):
    block = jnp.where(lax.axis_index(axis) == holder, block, jnp.zeros_like(block))
    return lax.psum(block, axis)


def per_device(h_old, s_old, row_owner, col_owner):
    row_count = lax.axis_size("row")
    col_count = lax.axis_size("col")
    old_rows = 2 * row_count
    old_cols = col_count // 2
    row_id = lax.axis_index("row")
    col_id = lax.axis_index("col")
    local_h = h_old[0, 0]
    local_s = s_old[0, 0]
    rows_here, cols_here = local_h.shape
    part_rows = rows_here // row_count
    part_cols = cols_here // col_count
    band = ORDER // row_count
    strip = ORDER // col_count
    panel_local = local_s.shape[1]
    rounds_row = part_rows // BLOCK
    rounds_col = part_cols // BLOCK
    span_row = rounds_row * old_rows
    span_col = rounds_col * old_cols
    owner_row = lax.dynamic_slice_in_dim(row_owner, row_id * span_row, span_row)[:, None]
    owner_col = lax.dynamic_slice_in_dim(col_owner, col_id * span_col, span_col)[None, :]
    round_row = (jnp.arange(span_row, dtype=jnp.int32) // old_rows)[:, None]
    round_col = (jnp.arange(span_col, dtype=jnp.int32) // old_cols)[None, :]
    outgoing = local_h.reshape(row_count, part_rows, col_count, part_cols).transpose(0, 2, 1, 3)
    received = several_exchanges(
        outgoing.reshape(row_count * col_count, part_rows, part_cols), ("row", "col"), 2, 0, 0
    )
    grid_h = received.reshape(row_count, col_count, rounds_row, BLOCK, rounds_col, BLOCK)
    shape_two = (span_row, span_col)
    source_row = jnp.broadcast_to(owner_row // 2, shape_two)
    source_col = 2 * owner_col + owner_row % 2
    picked = grid_h[
        source_row,
        source_col,
        jnp.broadcast_to(round_row, shape_two),
        :,
        jnp.broadcast_to(round_col, shape_two),
        :,
    ]
    h_block = picked.transpose(0, 2, 1, 3).reshape(band, strip)
    panel_blocks = PANEL // BLOCK
    panel_shape = (span_row, panel_blocks)
    panel_owner = col_owner[:panel_blocks][None, :]
    panel_slot = jnp.broadcast_to(
        (jnp.arange(panel_blocks, dtype=jnp.int32) // old_cols)[None, :], panel_shape
    )
    gather_col = 2 * panel_owner + owner_row % 2
    gather_row = jnp.broadcast_to(owner_row // 2, panel_shape)
    gather_round = jnp.broadcast_to(round_row, panel_shape)

    def arrange(gathered):
        grid_panel = gathered.reshape(
            col_count, row_count, rounds_row, BLOCK, panel_local // BLOCK, BLOCK
        )
        chosen = grid_panel[gather_col, gather_row, gather_round, :, panel_slot, :]
        return chosen.transpose(0, 2, 1, 3).reshape(band, PANEL)

    s_pieces = local_s.reshape(row_count, part_rows, panel_local)
    h_pieces = local_h[:, :panel_local].reshape(row_count, part_rows, panel_local)
    s_rows, h_rows = sent_together((s_pieces, h_pieces), "row", 0, 0, 1)
    s_all, h_all = (
        lax.all_gather(s_rows[None], "col", axis=0, tiled=True),
        lax.all_gather(h_rows[None], "col", axis=0, tiled=True),
    )
    s_panel = arrange(s_all)
    h_panel = arrange(h_all)
    corner_s, corner_h = (
        broadcast(s_panel[:PANEL], "row", 0),
        broadcast(h_panel[:PANEL], "row", 0),
    )
    lower_factor = jnp.linalg.cholesky(corner_s)
    solved = lax.linalg.triangular_solve(lower_factor, s_panel.T, left_side=True, lower=True)
    panel_factor = solved.T
    coupling = lax.linalg.triangular_solve(
        lower_factor, solved, left_side=True, lower=True, transpose_a=True
    ).T
    identity = jnp.eye(PANEL, dtype=jnp.float32)
    inverse = lax.linalg.triangular_solve(lower_factor, identity, left_side=True, lower=True)
    top_rows = jnp.concatenate(
        [identity - inverse, jnp.zeros((band - PANEL, PANEL), jnp.float32)], 0
    )
    leading = jnp.logical_and(row_id == 0, jnp.arange(band, dtype=jnp.int32)[:, None] < PANEL)
    coupling = jnp.where(leading, top_rows, coupling)
    mixed = h_panel - 0.5 * jnp.dot(coupling, corner_h, precision=lax.Precision.HIGHEST)
    offset = col_id * strip % band
    root_row = col_id * strip // band
    column_n, column_q = (
        broadcast(lax.dynamic_slice_in_dim(coupling, offset, strip), "row", root_row),
        broadcast(lax.dynamic_slice_in_dim(mixed, offset, strip), "row", root_row),
    )
    left_terms = jnp.concatenate([coupling, mixed], 1)
    right_terms = jnp.concatenate([column_q, column_n], 1)
    update = lax.dot_general(
        left_terms,
        right_terms,
        (((1,), (1,)), ((), ())),
        precision=lax.Precision.HIGHEST,
        preferred_element_type=jnp.float32,
    )
    return (h_block - update, panel_factor)


def solution(mesh):
    in_specs = (P("row", "col", None, None), P("row", "col", None, None), P(), P())
    out_specs = (P("row", "col"), P("row", None))
    return jax.shard_map(
        per_device, mesh=mesh, in_specs=in_specs, out_specs=out_specs, check_vma=False
    )
```

profile of v0, /device:TPU:1, one launch (start us, length us, event | category | flops | bytes accessed | tf_op | source)
XLA Modules:
  0.0 752.1 jit_solution(13469007670536325657)
XLA Ops:
  9.7 14.3 %all_to_all.15 = f32[8,256,64]{1,2,0:T(8,128)S(1)} all-to-all(f32[8,256,64]{1,2,0:T(8,128)S(1)} %copy.67), channel_id=1, replica_groups=mesh['row'=8,'col'=16] {'row'}, dimensions={0} | all-to-all | bytes 1048576 | tf_op jit(solution)/shard_map/all_to_all | solution.py:45
  26.1 56.3 %all-gather.5.cloned.1.call-done = f32[128,128,64]{1,2,0:T(8,128)} async-done(((f32[8,128,64]{1,2,0:T(8,128)}), f32[128,128,64]{1,2,0:T(8,128)}) %all-gather.5.cloned.1.call-update) | async-done | bytes 4194320 | tf_op jit(solution)/shard_map/all_gather | solution.py:118
  82.4 6.9 copy.68
  89.3 9.0 %gather_fusion.1 = f32[256,64,64]{2,1,0:T(8,128)} fusion(f32[16,8,2,64,1,64]{5,3,4,2,1,0:T(8,128)} %bitcast.134, s32[256]{0:T(256)S(1)} %reshape.649), kind=kCustom, calls=%fused_computation.1 | custom fusion | bytes 8392704 | tf_op jit(solution)/shard_map/gather | solution.py:111
  98.3 3.2 slice_select_fusion.1
  105.0 32.6 %all-gather.7.cloned.1.call-done = f32[128,128,64]{1,2,0:T(8,128)} async-done(((f32[8,128,64]{1,2,0:T(8,128)}), f32[128,128,64]{1,2,0:T(8,128)}) %all-gather.7.cloned.1.call-update) | async-done | bytes 4194320 | tf_op jit(solution)/shard_map/all_gather | solution.py:119
  137.6 6.9 copy.77
  144.5 8.8 %gather_fusion.2 = f32[256,64,64]{2,1,0:T(8,128)} fusion(f32[16,8,2,64,1,64]{5,3,4,2,1,0:T(8,128)} %bitcast.133, s32[256]{0:T(256)S(1)} %reshape.649), kind=kCustom, calls=%fused_computation.2 | custom fusion | bytes 8392704 | tf_op jit(solution)/shard_map/gather | solution.py:111
  157.8 5.4 copy.87
  163.8 2.5 copy.61
  166.3 4.2 slice_bitcast_fusion.1
  170.5 6.0 all-to-all-start.1
  178.6 9.5 %copy.85 = f32[32,64,8,64]{1,0,3,2:T(8,128)} copy(f32[32,64,8,64]{3,1,2,0:T(8,128)} %bitcast.129) | data formatting | bytes 8388608 | tf_op jit(solution)/shard_map/reshape | solution.py:112
  188.1 14.3 %copy.78 = f32[32,64,8,64]{3,2,1,0:T(8,128)} copy(f32[32,64,8,64]{3,1,2,0:T(8,128)} %bitcast.131) | data formatting | bytes 8388608 | tf_op jit(solution)/shard_map/transpose | solution.py:112
  202.4 7.8 %reshape.665 = f32[2048,512]{0,1:T(8,128)} reshape(f32[32,64,8,64]{1,0,3,2:T(8,128)} %copy.85) | data formatting | bytes 8388608 | tf_op jit(solution)/shard_map/reshape | solution.py:112
  210.2 7.6 %reshape.623 = f32[2048,512]{1,0:T(8,128)} reshape(f32[32,64,8,64]{3,2,1,0:T(8,128)} %copy.78) | data formatting | bytes 8388608 | tf_op jit(solution)/shard_map/reshape | solution.py:112
  217.9 85.3 %all-reduce.9.cloned.1.call-done = (f32[512,512]{0,1:T(8,128)}, f32[512,512]{1,0:T(8,128)}) async-done(((f32[512,512]{0,1:T(8,128)}, f32[512,512]{1,0:T(8,128)}), (f32[512,512]{0,1:T(8,128)}, f32[512,512]{1,0:T(8,128)})) %all-reduce.9.cloned.1.call-update) | async-done | bytes 2097168 | tf_op jit(solution)/shard_map/psum | solution.py:54
  306.2 11.7 %cholesky.103 = f32[128,128]{1,0:T(8,128)S(1)} custom-call(f32[128,128]{1,0:T(8,128)S(1)} %cholesky.263), custom_call_target="Cholesky" | custom-call | tf_op jit(solution)/shard_map/jit(cholesky)/cholesky | solution.py:127
  318.1 9.8 %custom-call.34 = f32[1,128,128]{1,2,0:T(8,128)S(1)} custom-call(f32[1,128,128]{2,1,0:T(8,128)S(1)} %get-tuple-element.50), custom_call_target="InvertDiagBlocksLowerTriangular" | custom-call | tf_op jit(solution)/shard_map/jit(cholesky)/cholesky | solution.py:127
  328.6 11.7 %cholesky.215 = f32[128,128]{1,0:T(8,128)S(1)} custom-call(f32[128,128]{1,0:T(8,128)S(1)} %cholesky.267), custom_call_target="Cholesky" | custom-call | tf_op jit(solution)/shard_map/jit(cholesky)/cholesky | solution.py:127
  340.3 10.2 %custom-call.35 = f32[1,128,128]{1,2,0:T(8,128)S(1)} custom-call(f32[1,128,128]{2,1,0:T(8,128)S(1)} %get-tuple-element.47), custom_call_target="InvertDiagBlocksLowerTriangular" | custom-call | tf_op jit(solution)/shard_map/jit(cholesky)/cholesky | solution.py:127
  351.2 11.7 %cholesky.236 = f32[128,128]{1,0:T(8,128)S(1)} custom-call(f32[128,128]{1,0:T(8,128)S(1)} %cholesky.272), custom_call_target="Cholesky" | custom-call | tf_op jit(solution)/shard_map/jit(cholesky)/cholesky | solution.py:127
  362.9 9.8 %custom-call.36 = f32[1,128,128]{1,2,0:T(8,128)S(1)} custom-call(f32[1,128,128]{2,1,0:T(8,128)S(1)} %get-tuple-element.44), custom_call_target="InvertDiagBlocksLowerTriangular" | custom-call | tf_op jit(solution)/shard_map/jit(cholesky)/cholesky | solution.py:127
  373.3 11.7 %cholesky.253 = f32[128,128]{1,0:T(8,128)S(1)} custom-call(f32[128,128]{1,0:T(8,128)S(1)} %convolution_subtract_fusion.9), custom_call_target="Cholesky" | custom-call | tf_op jit(solution)/shard_map/jit(cholesky)/cholesky | solution.py:127
  390.6 8.2 %while.1 = (s32[]{:T(128)}, f32[512,512]{1,0:T(8,128)S(1)}, s32[4,2]{0,1:T(2,128)S(1)}, f32[4,128,128]{2,1,0:T(8,128)S(1)}, s32[]{:T(128)}) while((s32[]{:T(128)}, f32[512,512]{1,0:T(8,128)S(1)}, s32[4,2]{0,1:T(2,128)S(1)}, f32[4,128,128]{2,1,0:T(8,128)S(1)}, s32[]{:T(128)}) %tuple.43), condition=%wide.while_cond, body=%wide.while_body.sunk | while | flops 2 | bytes 131189 | solution.py:134
  398.8 39.3 %custom-call.37 = f32[4,128,128]{1,2,0:T(8,128)S(1)} custom-call(f32[4,128,128]{2,1,0:T(8,128)S(1)} %get-tuple-element.9), custom_call_target="InvertDiagBlocksLowerTriangular" | custom-call | tf_op jit(solution)/shard_map/triangular_solve | solution.py:134
  438.1 2.4 fusion.37
  440.5 2.2 convolution_subtract_fusion.3
  446.2 3.2 fusion.28
  453.7 2.3 convolution_subtract_fusion.2
  458.0 2.5 copy.75
  460.6 2.8 convolution_subtract_fusion
  465.4 2.5 copy.74
  475.1 3.1 fusion.25
  480.8 2.1 copy-done
  484.5 10.7 %all-to-all-start = ((f32[128,1,64,128]{3,2,1,0:T(8,128)}), f32[128,1,64,128]{3,2,1,0:T(8,128)}, u32[]{:S(2)}, u32[]{:S(2)}) async-start(f32[128,1,64,128]{3,2,1,0:T(8,128)} %get-tuple-element.37), calls=%async_computation | async-start | bytes 8388608 | tf_op jit(solution)/shard_map/all_to_all | solution.py:33
  495.3 9.5 %multiply_subtract_fusion = f32[2048,512]{1,0:T(8,128)S(1)} fusion(f32[2048,512]{1,0:T(8,128)} %reshape.623, f32[2048,512]{1,0:T(8,128)} %copy-done, f32[512,512]{1,0:T(8,128)S(1)} %copy-done.12), kind=kOutput, calls=%fused_computation.19 | convolution fusion | flops 6444548096 | bytes 13631488 | tf_op jit(solution)/shard_map/dot_general | solution.py:140
  508.6 48.7 %all-to-all-done = f32[128,1,64,128]{3,2,1,0:T(8,128)} async-done(((f32[128,1,64,128]{3,2,1,0:T(8,128)}), f32[128,1,64,128]{3,2,1,0:T(8,128)}, u32[]{:S(2)}, u32[]{:S(2)}) %all-to-all-start) | async-done | bytes 4194336 | tf_op jit(solution)/shard_map/all_to_all | solution.py:33
  557.4 8.1 %pad_maximum_fusion = f32[128,1,128,128]{3,2,1,0:T(8,128)} fusion(f32[128,1,64,128]{3,2,1,0:T(8,128)} %all-to-all-done.1, f32[128,1,64,128]{3,2,1,0:T(8,128)} %all-to-all-done), kind=kLoop, calls=%fused_computation.6 | loop fusion | flops 2097152 | bytes 16777216 | tf_op jit(solution)/shard_map/concatenate | solution.py:34
  565.5 16.9 %reshape_reshape.7 = f32[8,16,2,64,2,64]{5,4,3,2,1,0:T(2,128)} reshape(f32[128,1,128,128]{3,2,1,0:T(8,128)} %pad_maximum_fusion) | data formatting | bytes 16777216 | tf_op jit(solution)/shard_map/reshape;reshape | solution.py:84
  582.4 12.7 %copy.64 = f32[8,16,2,64,2,64]{5,3,4,2,1,0:T(8,128)} copy(f32[8,16,2,64,2,64]{5,4,3,2,1,0:T(2,128)} %reshape_reshape.7) | data formatting | bytes 16777216 | tf_op jit(solution)/shard_map/reshape;reshape | solution.py:84
  595.1 16.8 %gather_fusion = f32[512,64,64]{2,1,0:T(8,128)} fusion(f32[8,16,2,64,2,64]{5,3,4,2,1,0:T(8,128)} %copy.64, s32[512]{0:T(512)S(1)} %reshape.643), kind=kCustom, calls=%fused_computation | custom fusion | bytes 16785408 | tf_op jit(solution)/shard_map/gather | solution.py:88
  611.9 18.5 %copy.65 = f32[32,64,16,64]{3,2,1,0:T(8,128)} copy(f32[32,64,16,64]{3,1,2,0:T(8,128)} %bitcast.127) | data formatting | bytes 16777216 | tf_op jit(solution)/shard_map/transpose | solution.py:96
  630.4 14.9 %reshape.618 = f32[2048,1024]{1,0:T(8,128)} reshape(f32[32,64,16,64]{3,2,1,0:T(8,128)} %copy.65) | data formatting | bytes 16777216 | tf_op jit(solution)/shard_map/reshape | solution.py:96
  645.3 3.5 maximum_bitcast_fusion.1
  648.8 5.3 copy.81
  654.2 58.7 %all-reduce.7.cloned.1.call-done = (f32[1024,512]{1,0:T(8,128)}, f32[1024,512]{1,0:T(8,128)}) async-done(((f32[1024,512]{1,0:T(8,128)}, f32[1024,512]{1,0:T(8,128)}), (f32[1024,512]{1,0:T(8,128)}, f32[1024,512]{1,0:T(8,128)})) %all-reduce.7.cloned.1.call-update) | async-done | bytes 4194320 | tf_op jit(solution)/shard_map/psum | solution.py:54
  712.9 32.5 %fusion.8 = f32[2048,1024]{1,0:T(8,128)} fusion(f32[2048,1024]{1,0:T(8,128)} %reshape.618, f32[1024,512]{1,0:T(8,128)} %get-tuple-element.28, f32[1024,512]{1,0:T(8,128)} %get-tuple-element.29, f32[2048,512]{1,0:T(8,128)} %copy-done.5, f32[2048,512]{1,0:T(8,128)} %copy-done), kind=kOutput, calls=%fused_computation.20 | convolution fusion | flops 25775046656 | bytes 29360128 | tf_op jit(solution)/shard_map/dot_general | solution.py:149
  (123 shorter events, 57.9 us)
Async XLA Ops:
  7.2 18.6 %copy-start.13 = (s32[256]{0:T(256)S(1)}, s32[256]{0:T(256)}, u32[]{:S(2)}) copy-start(s32[256]{0:T(256)} %param.6) | copy-start | bytes 3076
  7.2 18.7 %copy-start.14 = (s32[256]{0:T(256)S(1)}, s32[256]{0:T(256)}, u32[]{:S(2)}) copy-start(s32[256]{0:T(256)} %param.7) | copy-start | bytes 3076
  7.2 75.2 %all-gather.5.cloned.1.call-start = ((), (), s32[]{:S(2)}) async-start(), calls=%async_computation.3 | async-start | bytes 4456448 | tf_op jit(solution)/shard_map/all_gather | solution.py:118
  24.9 112.7 %all-gather.7.cloned.1.call-start = ((), (), s32[]{:S(2)}) async-start(), calls=%async_computation.4 | async-start | bytes 4456448 | tf_op jit(solution)/shard_map/all_gather | solution.py:119
  25.7 277.5 %all-reduce.9.cloned.1.call-start = ((), (), s32[]{:S(2)}) async-start(), calls=%async_computation.6 | async-start | bytes 4194304 | tf_op jit(solution)/shard_map/psum | solution.py:54
  170.5 314.0 %all-to-all-start.1 = ((f32[128,1,64,128]{3,2,1,0:T(8,128)}), f32[128,1,64,128]{3,2,1,0:T(8,128)}, u32[]{:S(2)}, u32[]{:S(2)}) async-start(f32[128,1,64,128]{3,2,1,0:T(8,128)} %get-tuple-element.38), calls=%async_computation.1 | async-start | bytes 8388608 | tf_op jit(solution)/shard_map/all_to_all | solution.py:33
  398.8 45.1 %copy-start.8 = (f32[512,512]{1,0:T(8,128)}, f32[512,512]{1,0:T(8,128)S(1)}, u32[]{:S(2)}) copy-start(f32[512,512]{1,0:T(8,128)S(1)} %get-tuple-element.122) | copy-start | bytes 3145732
  438.1 5.7 copy-start.1
  446.2 3.2 copy-start.3
  450.4 1.0 copy-start.7
  467.9 7.2 copy-start.2
  467.9 7.2 copy-start.6
  475.1 5.0 copy-start.9
  475.1 5.0 copy-start.10
  475.1 5.0 copy-start.11
  480.8 2.1 copy-start
  484.5 10.8 %copy-start.12 = (f32[512,512]{1,0:T(8,128)S(1)}, f32[512,512]{1,0:T(8,128)}, u32[]{:S(2)}) copy-start(f32[512,512]{1,0:T(8,128)} %get-tuple-element.31) | copy-start | bytes 3145732
  484.5 72.9 %all-to-all-start = ((f32[128,1,64,128]{3,2,1,0:T(8,128)}), f32[128,1,64,128]{3,2,1,0:T(8,128)}, u32[]{:S(2)}, u32[]{:S(2)}) async-start(f32[128,1,64,128]{3,2,1,0:T(8,128)} %get-tuple-element.37), calls=%async_computation | async-start | bytes 8388608 | tf_op jit(solution)/shard_map/all_to_all | solution.py:33
  495.2 217.7 %all-reduce.7.cloned.1.call-start = ((), (), s32[]{:S(2)}) async-start(), calls=%async_computation.5 | async-start | bytes 8388608 | tf_op jit(solution)/shard_map/psum | solution.py:54
  504.8 2.0 copy-start.5
  630.4 14.9 %copy-start.4 = (f32[128,2048]{1,0:T(8,128)S(1)}, f32[128,2048]{1,0:T(8,128)}, u32[]{:S(2)}) copy-start(f32[128,2048]{1,0:T(8,128)} %copy-done.3) | copy-start | bytes 3145732
Sparse Core Ops, SparseCore 0:
  25.1 57.3 all-gather.4
  84.9 52.6 all-gather.6
  157.9 145.1 all-reduce.8
  508.5 204.3 all-reduce.6
where the time goes:
time: 763 us; the launch traced here: 752 us
  waiting for transfers between devices  282 us (37%)
  local copies, waits for them, and re-layouts  200 us (26%)
  other arithmetic  143 us (19%)
  matrix products  78.2 us (10%)
  between operations  17.2 us (2%)
  starting transfers between devices  16.9 us (2%)
  blocking collectives  14.3 us (2%)
    psum x2, waiting for transfers between devices, broadcast(): return lax.psum(block, axis)  144 us
    another operation x15, other arithmetic, per_device(): lower_factor = jnp.linalg.cholesky(corner_s)  79.5 us
    all_gather x1, waiting for transfers between devices, per_device(): lax.all_gather(s_rows[None], 'col', axis=0, tiled=True)  56.3 us
    all_to_all x2, waiting for transfers between devices, several_exchanges(): lax.all_to_all(share, axis, split_axis=0, concat_axis=0, tiled=True)  48.7 us
    another operation x3, other arithmetic, per_device(): lax.linalg.triangular_solve(lower_factor, identity, left_side=True, lower...  39.6 us
    all_gather x1, waiting for transfers between devices, per_device(): lax.all_gather(h_rows[None], 'col', axis=0, tiled=True)  32.6 us
    dot_general x1, matrix products, per_device(): lax.dot_general(left_terms, right_terms, (((1,), (1,)), ((), ())), precis...  32.5 us
    another operation x2, local copies, waits for them, and re-layouts, per_device(): received.reshape(row_count, col_count, rounds_row, BLOCK, rounds_col, BLOCK)  29.7 us
  transfers between devices with their start and end apart: 6, of which 5 were waited for; matrix products, arithmetic and copies ran while one was open for 48% of the time, Pallas kernels for 0%

commit v1 on v0

v1 whole, which is shorter than its diff:
```python
import jax
import jax.numpy as jnp
from jax import lax
from jax.experimental import pallas as pl
from jax.experimental.pallas import tpu as pltpu
from jax.sharding import PartitionSpec as P

ORDER = 16384
PANEL = 512
BLOCK = 64
STEP = 128
HIGHEST = lax.Precision.HIGHEST
BF16 = jnp.bfloat16
F32 = jnp.float32


def dot(a, b, ca, cb, precision=None):
    return lax.dot_general(
        a, b, (((ca,), (cb,)), ((), ())), precision=precision, preferred_element_type=F32
    )


def halves(x):
    high = x.astype(BF16)
    return high, (x - high.astype(F32)).astype(BF16)


def lower_half(shape):
    return lax.broadcasted_iota(jnp.int32, shape, 1) < BLOCK


def fetch_panel(read, rows, first, row_owner, col_owner, s_out, h_out):
    low = lower_half((BLOCK, 2 * BLOCK))
    for i in range(rows):
        p = row_owner[first + i]
        for k in range(0, PANEL // BLOCK, 2):
            one = read(i, p, col_owner[k])
            two = read(i, p, col_owner[k + 1])
            at = (pl.ds(i * BLOCK, BLOCK), pl.ds(k * BLOCK, 2 * BLOCK))
            s_out[at] = jnp.where(low, one, pltpu.roll(two, BLOCK, 1))
            h_out[at] = jnp.where(low, pltpu.roll(one, BLOCK, 1), two)


def spread(x, rows):
    return jnp.broadcast_to(x, (rows, x.shape[1]))


def factor_inverse(a_ref, b_ref):
    sub = lax.broadcasted_iota(jnp.int32, (8, STEP), 0)
    for j in range(0, STEP, 8):
        far = STEP - j - 8
        a_near, b_near = a_ref[j : j + 8, :], b_ref[j : j + 8, :]
        near = [jnp.broadcast_to(a_near[:, j + t : j + t + 1], (8, STEP)) for t in range(8)]
        if far:
            a_far, b_far = a_ref[j + 8 :, :], b_ref[j + 8 :, :]
            cols = [jnp.broadcast_to(a_far[:, j + t : j + t + 1], (far, STEP)) for t in range(8)]
        scales, links = [], []
        for t in range(8):
            r = lax.rsqrt(near[t][t : t + 1, :])
            l = near[t] * spread(r, 8)
            below = jnp.where(sub > t, l, 0.0)
            a_row, b_row = a_near[t : t + 1, :] * r, b_near[t : t + 1, :] * r
            a_near = jnp.where(sub == t, spread(a_row, 8), a_near - below * spread(a_row, 8))
            b_near = jnp.where(sub == t, spread(b_row, 8), b_near - below * spread(b_row, 8))
            link = {}
            for u in range(t + 1, 8):
                link[u] = l[u : u + 1, :]
                near[u] = near[u] - l * spread(link[u], 8)
            scales.append(r)
            links.append(link)
        b_ref[j : j + 8, :] = b_near
        if far:
            for t in range(8):
                l = cols[t] * spread(scales[t], far)
                for u in range(t + 1, 8):
                    cols[u] = cols[u] - l * spread(links[t][u], far)
                a_far = a_far - l * spread(a_near[t : t + 1, :], far)
                b_far = b_far - l * spread(b_near[t : t + 1, :], far)
            a_ref[j + 8 :, :] = a_far
            b_ref[j + 8 :, :] = b_far


def corner_kernel(row_owner, col_owner, tiles, inverse, corner_h, s_top, work, a_blk, b_blk):
    fetch_panel(
        lambda i, p, q: tiles[2 * q + p % 2, p // 2],
        PANEL // BLOCK, 0, row_owner, col_owner, s_top, corner_h,
    )
    eye = lax.broadcasted_iota(jnp.int32, (STEP, STEP), 0) == lax.broadcasted_iota(
        jnp.int32, (STEP, STEP), 1
    )
    eye = jnp.where(eye, 1.0, 0.0)
    count = PANEL // STEP
    for k in range(count):
        work[k, :, :PANEL] = s_top[k * STEP : (k + 1) * STEP, :]
        work[k, :, PANEL:] = jnp.zeros((STEP, PANEL), F32)
        work[k, :, PANEL + k * STEP : PANEL + (k + 1) * STEP] = eye
    lane = lax.broadcasted_iota(jnp.int32, (STEP, PANEL), 1)

    def step(k, carry):
        a_blk[...] = work[k, :, pl.ds(pl.multiple_of(k * STEP, STEP), STEP)]
        b_blk[...] = eye
        factor_inverse(a_blk, b_blk)
        rows = dot(b_blk[...], work[k], 1, 0, HIGHEST)
        work[k] = rows
        ahead = jnp.where(lane >= (k + 1) * STEP, rows[:, :PANEL], 0.0).T
        for i in range(1, count):
            work[i] = work[i] - dot(ahead[i * STEP : (i + 1) * STEP], rows, 1, 0, HIGHEST)
        return carry

    lax.fori_loop(0, count, step, 0)
    for k in range(count):
        inverse[k * STEP : (k + 1) * STEP, :] = work[k, :, PANEL:]


def coupling_of(s_rows, inverse, special):
    factor = dot(s_rows, inverse, 1, 1, HIGHEST)
    coupling = dot(factor, inverse, 1, 0, HIGHEST)
    shape = (PANEL, PANEL)
    eye = lax.broadcasted_iota(jnp.int32, shape, 0) == lax.broadcasted_iota(jnp.int32, shape, 1)
    return factor, jnp.where(special, jnp.where(eye, 1.0, 0.0) - inverse, coupling)


def strip_kernel(place, row_owner, col_owner, tiles, inv, corner_h, high, low, s_buf, h_buf):
    step = pl.program_id(0)
    here = place[1]
    fetch_panel(
        lambda i, p, q: tiles[p // 2, 2 * q + p % 2],
        PANEL // BLOCK, here * 16 + step * 8, row_owner, col_owner, s_buf, h_buf,
    )
    special = jnp.logical_and(here == 0, step == 0)
    _, coupling = coupling_of(s_buf[...], inv[...], special)
    rest = h_buf[...] - dot(coupling, corner_h[...], 1, 0, HIGHEST)
    high[:, :PANEL], low[:, :PANEL] = halves(rest)
    high[:, PANEL:], low[:, PANEL:] = halves(coupling)


def band_kernel(place, row_owner, col_owner, tiles, inv, factor, high, low, s_buf, h_buf):
    step = pl.program_id(0)
    here = place[0]
    slot = pl.multiple_of((step // 2) * BLOCK, BLOCK)
    fetch_panel(
        lambda i, p, q: tiles[2 * q + p % 2, p // 2, pl.ds(slot, BLOCK), :],
        PANEL // BLOCK, here * 32 + step * 8, row_owner, col_owner, s_buf, h_buf,
    )
    special = jnp.logical_and(here == 0, step == 0)
    factor[...], coupling = coupling_of(s_buf[...], inv[...], special)
    high[:, :PANEL], low[:, :PANEL] = halves(coupling)
    high[:, PANEL:], low[:, PANEL:] = halves(h_buf[...])


def final_kernel(place, row_owner, col_owner, tiles, lh, ll, rh, rl, out):
    step = pl.program_id(0)
    blocks = out.shape[0] // BLOCK
    update = dot(lh[...], rh[...], 1, 1)
    update = update + dot(lh[...], rl[...], 1, 1)
    update = update + dot(ll[...], rh[...], 1, 1)
    out[...] = update
    low = lower_half((BLOCK, 2 * BLOCK))
    slot = pl.multiple_of((step * blocks // 16) * BLOCK, BLOCK)
    for i in range(blocks):
        p = row_owner[place[0] * 32 + step * blocks + i]
        for j in range(0, 16, 2):
            one = tiles[p // 2, 2 * col_owner[place[1] * 16 + j] + p % 2, pl.ds(slot, BLOCK), :]
            two = tiles[p // 2, 2 * col_owner[place[1] * 16 + j + 1] + p % 2, pl.ds(slot, BLOCK), :]
            if j < 8:
                both = jnp.where(low, one, pltpu.roll(two, BLOCK, 1))
            else:
                both = jnp.where(low, pltpu.roll(one, BLOCK, 1), two)
            at = (pl.ds(i * BLOCK, BLOCK), pl.ds(j * BLOCK, 2 * BLOCK))
            out[at] = both - out[at]


def whole(shape):
    return pl.BlockSpec(shape, lambda *i: (0,) * len(shape), pipeline_mode=pl.Buffered(1))


SMEM = pl.BlockSpec(memory_space=pltpu.SMEM)
LIMIT = pltpu.CompilerParams(vmem_limit_bytes=60 * 2**20)


def shape_of(shape, dtype=F32):
    return jax.ShapeDtypeStruct(shape, dtype)


def per_device(h_old, s_old, row_owner, col_owner):
    rows_n = lax.axis_size("row")
    cols_n = lax.axis_size("col")
    row_id = lax.axis_index("row")
    col_id = lax.axis_index("col")
    place = jnp.stack([row_id, col_id]).astype(jnp.int32)
    local_h = h_old[0, 0]
    local_s = s_old[0, 0]
    band = ORDER // rows_n
    strip = ORDER // cols_n
    panels = jnp.concatenate([local_s, local_h[:, :BLOCK]], axis=1)

    top = lax.all_gather(panels[:BLOCK], "row", axis=0)
    top = lax.all_gather(top, "col", axis=0)
    inverse, corner_h = pl.pallas_call(
        corner_kernel,
        out_shape=(shape_of((PANEL, PANEL)), shape_of((PANEL, PANEL))),
        in_specs=[SMEM, SMEM, pl.BlockSpec(memory_space=pltpu.VMEM)],
        scratch_shapes=[
            pltpu.VMEM((PANEL, PANEL), F32),
            pltpu.VMEM((PANEL // STEP, STEP, 2 * PANEL), F32),
            pltpu.VMEM((STEP, STEP), F32),
            pltpu.VMEM((STEP, STEP), F32),
        ],
        compiler_params=LIMIT,
        cost_estimate=pl.CostEstimate(flops=3 * 10**10, bytes_accessed=6 * 2**20, transcendentals=0),
        name="corner",
    )(row_owner, col_owner, top)

    band_tiles = lax.all_to_all(panels.reshape(rows_n, 128, 128), "row", 0, 0, tiled=True)
    band_tiles = lax.all_gather(band_tiles, "col", axis=0)
    strip_tiles = lax.all_to_all(panels.reshape(cols_n, BLOCK, 128), "col", 0, 0, tiled=True)
    strip_tiles = lax.all_gather(strip_tiles, "row", axis=0)

    outgoing = local_h.reshape(rows_n, 128, cols_n, 128).transpose(0, 2, 1, 3)
    h_tiles = lax.all_to_all(
        outgoing.reshape(rows_n * cols_n, 128, 128), ("row", "col"), 0, 0, tiled=True
    ).reshape(rows_n, cols_n, 128, 128)

    buffers = [pltpu.VMEM((PANEL, PANEL), F32), pltpu.VMEM((PANEL, PANEL), F32)]
    right_high, right_low = pl.pallas_call(
        strip_kernel,
        grid=(strip // PANEL,),
        out_shape=(shape_of((strip, 2 * PANEL), BF16),) * 2,
        in_specs=[SMEM, SMEM, SMEM, whole(strip_tiles.shape), whole((PANEL, PANEL)), whole((PANEL, PANEL))],
        out_specs=(pl.BlockSpec((PANEL, 2 * PANEL), lambda i: (i, 0)),) * 2,
        scratch_shapes=buffers,
        compiler_params=LIMIT,
        cost_estimate=pl.CostEstimate(flops=10**10, bytes_accessed=10 * 2**20, transcendentals=0),
        name="strip",
    )(place, row_owner, col_owner, strip_tiles, inverse, corner_h)

    factor, left_high, left_low = pl.pallas_call(
        band_kernel,
        grid=(band // PANEL,),
        out_shape=(shape_of((band, PANEL)),) + (shape_of((band, 2 * PANEL), BF16),) * 2,
        in_specs=[SMEM, SMEM, SMEM, whole(band_tiles.shape), whole((PANEL, PANEL))],
        out_specs=(pl.BlockSpec((PANEL, PANEL), lambda i: (i, 0)),)
        + (pl.BlockSpec((PANEL, 2 * PANEL), lambda i: (i, 0)),) * 2,
        scratch_shapes=buffers,
        compiler_params=LIMIT,
        cost_estimate=pl.CostEstimate(flops=13 * 10**9, bytes_accessed=20 * 2**20, transcendentals=0),
        name="band",
    )(place, row_owner, col_owner, band_tiles, inverse)

    tall = 256
    h_block = pl.pallas_call(
        final_kernel,
        grid=(band // tall,),
        out_shape=shape_of((band, strip)),
        in_specs=[SMEM, SMEM, SMEM, whole(h_tiles.shape)]
        + [pl.BlockSpec((tall, 2 * PANEL), lambda i: (i, 0))] * 2
        + [whole((strip, 2 * PANEL))] * 2,
        out_specs=pl.BlockSpec((tall, strip), lambda i: (i, 0)),
        compiler_params=LIMIT,
        cost_estimate=pl.CostEstimate(flops=13 * 10**9, bytes_accessed=28 * 2**20, transcendentals=0),
        name="final",
    )(place, row_owner, col_owner, h_tiles, left_high, left_low, right_high, right_low)
    return h_block, factor


def solution(mesh):
    in_specs = (P("row", "col", None, None), P("row", "col", None, None), P(), P())
    out_specs = (P("row", "col"), P("row", None))
    return jax.shard_map(
        per_device, mesh=mesh, in_specs=in_specs, out_specs=out_specs, check_vma=False
    )
```

time: 763 us -> 394 us (0.52); the launches traced: 752 us -> 394 us
  local copies, waits for them, and re-layouts: 200 us -> 14.5 us
  other arithmetic: 143 us -> 1.08 us
  Pallas kernels: 0 us -> 81.9 us
  matrix products: 78.2 us -> 0 us
  waiting for transfers between devices: 282 us -> 210 us
  blocking collectives: 14.3 us -> 63.2 us
  starting transfers between devices: 16.9 us -> 9.08 us
    psum x2 -> x0, waiting for transfers between devices: 144 us -> none  [broadcast(): return lax.psum(block, axis)]
    all_gather x2 -> x3, waiting for transfers between devices: 88.9 us -> 210 us  [the longest x1 142 us: per_device(): strip_tiles = lax.all_gather(strip_tiles, 'row', axis=0)]
    another operation x18 -> x1, other arithmetic: 119 us -> 0.6 us  [per_device(): place = jnp.stack([row_id, col_id]).astype(jnp.int32)]
    pallas_call x0 -> x4, Pallas kernels: none -> 81.9 us  [the longest x1 25.9 us: per_device(): pl.pallas_call(corner_kernel, out_shape=(shape_of((PANEL, PANEL)), shape_...]
    all_to_all x2 -> x1, waiting for transfers between devices: 48.7 us -> 0.01 us  [per_device(): lax.all_to_all(outgoing.reshape(rows_n * cols_n, 128, 128), ('row', 'col'...]
    another operation x22 -> x0, local copies, waits for them, and re-layouts: 44.3 us -> none  [the longest x2 29.7 us: per_device(): received.reshape(row_count, col_count, rounds_row, BLOCK, rounds_col, BLOCK)]
    dot_general x2 -> x0, matrix products: 42.1 us -> none  [the longest x1 32.5 us: per_device(): lax.dot_general(left_terms, right_terms, (((1,), (1,)), ((), ())), precis...]
    reshape x5 -> x0, local copies, waits for them, and re-layouts: 40.1 us -> none  [the longest x3 25 us: arrange(): return chosen.transpose(0, 2, 1, 3).reshape(band, PANEL)]
  transfers between devices with their start and end apart: 6 -> 4, of which waited for: 5 -> 3; matrix products, arithmetic and copies ran while one was open for 48% -> 3% of each run, Pallas kernels for 0% -> 15%
where the time goes in v1:
time: 394 us
  waiting for transfers between devices  210 us (53%)
  Pallas kernels  81.9 us (21%)
  blocking collectives  63.2 us (16%)
  local copies, waits for them, and re-layouts  14.5 us (4%)
  between operations  13.8 us (4%)
  starting transfers between devices  9.08 us (2%)
    all_gather x1, waiting for transfers between devices, per_device(): strip_tiles = lax.all_gather(strip_tiles, 'row', axis=0)  142 us
    all_gather x1, waiting for transfers between devices, per_device(): band_tiles = lax.all_gather(band_tiles, 'col', axis=0)  64 us
    all_to_all x1, blocking collectives, per_device(): lax.all_to_all(panels.reshape(cols_n, BLOCK, 128), 'col', 0, 0, tiled=True)  27.5 us
    pallas_call x1, Pallas kernels, per_device(): pl.pallas_call(corner_kernel, out_shape=(shape_of((PANEL, PANEL)), shape_...  25.9 us
    all_gather x1, blocking collectives, per_device(): top = lax.all_gather(panels[:BLOCK], 'row', axis=0)  25 us
    pallas_call x1, Pallas kernels, per_device(): pl.pallas_call(final_kernel, grid=(band // tall,), out_shape=shape_of((ba...  20.9 us
    pallas_call x1, Pallas kernels, per_device(): pl.pallas_call(band_kernel, grid=(band // PANEL,), out_shape=(shape_of((b...  19.9 us
    pallas_call x1, Pallas kernels, per_device(): pl.pallas_call(strip_kernel, grid=(strip // PANEL,), out_shape=(shape_of(...  15.2 us
  transfers between devices with their start and end apart: 4, of which 3 were waited for; matrix products, arithmetic and copies ran while one was open for 3% of the time, Pallas kernels for 15%

profile of v1, /device:TPU:1, one launch (start us, length us, event | category | flops | bytes accessed | tf_op | source)
XLA Modules:
  0.0 393.9 jit_solution(9767471169567590451)
XLA Ops:
  7.2 0.0 all-gather.10.cloned.1.call-start
  7.2 1.1 slice.8
  8.3 1.1 copy.18
  9.4 0.1 pad_maximum_fusion.2
  9.5 25.0 %all-gather.1 = f32[512,128]{1,0:T(8,128)} all-gather(f32[64,128]{1,0:T(8,128)S(1)} %pad_maximum_fusion.2), channel_id=3, replica_groups=mesh['row'=8,'col'=16] {'row'}, dimensions={0}, use_global_device_ids=true | all-gather | bytes 294912 | tf_op jit(solution)/shard_map/all_gather | solution.py:197
  34.5 0.0 all-gather.10.cloned.1.call-update
  34.6 0.0 all-gather.12.cloned.1.call-start
  34.6 0.2 pad_maximum_fusion.1
  34.8 27.5 %all_to_all.15 = f32[16,64,128]{2,1,0:T(8,128)} all-to-all(f32[16,64,128]{2,1,0:T(8,128)S(1)} %pad_maximum_fusion.1), channel_id=1, replica_groups=mesh['row'=8,'col'=16] {'col'}, dimensions={0} | all-to-all | bytes 1048576 | tf_op jit(solution)/shard_map/all_to_all | solution.py:216
  62.4 0.0 all-gather.12.cloned.1.call-update
  62.4 0.0 all-gather.8.cloned.1.call-start
  62.4 0.2 pad_maximum_fusion
  62.6 10.7 %all_to_all.16 = f32[8,128,128]{2,1,0:T(8,128)} all-to-all(f32[8,128,128]{2,1,0:T(8,128)S(1)} %pad_maximum_fusion), channel_id=1, replica_groups=mesh['row'=8,'col'=16] {'row'}, dimensions={0} | all-to-all | bytes 1048576 | tf_op jit(solution)/shard_map/all_to_all | solution.py:214
  73.3 0.0 all-gather.8.cloned.1.call-update
  73.4 5.8 %copy.21 = f32[128,8,16,128]{3,2,1,0:T(8,128)S(1)} copy(f32[128,8,16,128]{3,1,2,0:T(8,128)} %bitcast.26) | data formatting | bytes 16777216
  79.2 0.5 bitcast_bitcast_fusion
  79.7 5.9 %copy.17 = f32[8,16,128,128]{3,2,1,0:T(8,128)} copy(f32[8,16,128,128]{3,1,2,0:T(8,128)S(1)} %bitcast_bitcast_fusion) | data formatting | bytes 16777216 | tf_op jit(solution)/shard_map/transpose | solution.py:219
  85.6 9.0 %all-to-all-start = ((f32[128,128,128]{2,1,0:T(8,128)}), f32[128,128,128]{2,1,0:T(8,128)}, u32[]{:S(2)}, u32[]{:S(2)}) async-start(f32[128,128,128]{2,1,0:T(8,128)} %bitcast.23), calls=%async_computation | async-start | bytes 16777216 | tf_op jit(solution)/shard_map/all_to_all | solution.py:220
  94.6 0.6 pad_add_fusion.place
  95.2 4.1 %all-gather.10.cloned.1.call-done = f32[128,64,128]{2,1,0:T(8,128)} async-done(((f32[8,64,128]{2,1,0:T(8,128)}), f32[128,64,128]{2,1,0:T(8,128)}) %all-gather.10.cloned.1.call-update) | async-done | bytes 4194320 | tf_op jit(solution)/shard_map/all_gather | solution.py:198
  99.3 25.9 %corner.1 = (f32[512,512]{1,0:T(8,128)}, f32[512,512]{1,0:T(8,128)}) custom-call(s32[256]{0:T(256)} %row_owner.7, s32[256]{0:T(256)} %col_owner.7, f32[16,8,64,128]{3,2,1,0:T(8,128)} %bitcast.34), custom_call_target="tpu_custom_call" | custom-call | flops 30000001024 | bytes 6291456 | tf_op jit(solution)/shard_map/corner/pallas_call | solution.py:199
  125.3 142.1 %all-gather.12.cloned.1.call-done = f32[128,64,128]{2,1,0:T(8,128)} async-done(((f32[16,64,128]{2,1,0:T(8,128)}), f32[128,64,128]{2,1,0:T(8,128)}) %all-gather.12.cloned.1.call-update) | async-done | bytes 4194320 | tf_op jit(solution)/shard_map/all_gather | solution.py:217
  267.4 15.2 %strip.1 = (bf16[1024,1024]{1,0:T(8,128)(2,1)}, bf16[1024,1024]{1,0:T(8,128)(2,1)}) custom-call(s32[2]{0:T(128)} %pad_add_fusion.place, s32[256]{0:T(256)} %row_owner.7, s32[256]{0:T(256)} %col_owner.7, f32[8,16,64,128]{3,2,1,0:T(8,128)} %bitcast.35, f32[512,512]{1,0:T(8,128)} %get-tuple-element.9.inv, f32[512,512]{1,0:T(8,128)} %get-tuple-element.12.corner_h), custom_call_target="tpu_custom_call" | custom-call | flops 10000000000 | bytes 10485760 | tf_op jit(solution)/shard_map/strip/pallas_call | solution.py:225
  282.6 64.0 %all-gather.8.cloned.1.call-done = f32[128,128,128]{2,1,0:T(8,128)} async-done(((f32[8,128,128]{2,1,0:T(8,128)}), f32[128,128,128]{2,1,0:T(8,128)}) %all-gather.8.cloned.1.call-update) | async-done | bytes 8388624 | tf_op jit(solution)/shard_map/all_gather | solution.py:215
  346.6 19.9 %band.1 = (f32[2048,512]{1,0:T(8,128)}, bf16[2048,1024]{1,0:T(8,128)(2,1)}, bf16[2048,1024]{1,0:T(8,128)(2,1)}) custom-call(s32[2]{0:T(128)} %pad_add_fusion.place, s32[256]{0:T(256)} %row_owner.7, s32[256]{0:T(256)} %col_owner.7, f32[16,8,128,128]{3,2,1,0:T(8,128)} %bitcast.33, f32[512,512]{1,0:T(8,128)} %get-tuple-element.9.inv), custom_call_target="tpu_custom_call" | custom-call | flops 12999999488 | bytes 20971520 | tf_op jit(solution)/shard_map/band/pallas_call | solution.py:237
  366.5 0.0 all-to-all-done
  366.5 20.9 %final.1 = f32[2048,1024]{1,0:T(8,128)} custom-call(s32[2]{0:T(128)} %pad_add_fusion.place, s32[256]{0:T(256)} %row_owner.7, s32[256]{0:T(256)} %col_owner.7, f32[8,16,128,128]{3,2,1,0:T(8,128)} %bitcast.4.tiles, bf16[2048,1024]{1,0:T(8,128)(2,1)} %get-tuple-element.10.lh, bf16[2048,1024]{1,0:T(8,128)(2,1)} %get-tuple-element.11.ll, ...), custom_call_target="tpu_custom_call" | custom-call | flops 12999999488 | bytes 29360128 | tf_op jit(solution)/shard_map/final/pallas_call | solution.py:251
Async XLA Ops:
  7.2 92.2 %all-gather.10.cloned.1.call-start = ((), (), s32[]{:S(2)}) async-start(), calls=%async_computation.4 | async-start | bytes 4456448 | tf_op jit(solution)/shard_map/all_gather | solution.py:198
  34.6 232.8 %all-gather.12.cloned.1.call-start = ((), (), s32[]{:S(2)}) async-start(), calls=%async_computation.5 | async-start | bytes 4718592 | tf_op jit(solution)/shard_map/all_gather | solution.py:217
  62.4 284.2 %all-gather.8.cloned.1.call-start = ((), (), s32[]{:S(2)}) async-start(), calls=%async_computation.3 | async-start | bytes 8912896 | tf_op jit(solution)/shard_map/all_gather | solution.py:215
  85.6 280.9 %all-to-all-start = ((f32[128,128,128]{2,1,0:T(8,128)}), f32[128,128,128]{2,1,0:T(8,128)}, u32[]{:S(2)}, u32[]{:S(2)}) async-start(f32[128,128,128]{2,1,0:T(8,128)} %bitcast.23), calls=%async_computation | async-start | bytes 16777216 | tf_op jit(solution)/shard_map/all_to_all | solution.py:220
Sparse Core Ops, SparseCore 0:
  34.7 64.5 all-gather.9
  101.0 166.3 all-gather.11
  269.8 76.6 all-gather.7

commit v2 on v1

--- a/solution.py
+++ b/solution.py
@@ -82,7 +82,7 @@
 
 def corner_kernel(row_owner, col_owner, tiles, inverse, corner_h, s_top, work, a_blk, b_blk):
     fetch_panel(
-        lambda i, p, q: tiles[2 * q + p % 2, p // 2],
+        lambda i, p, q: tiles[2 * q + p % 2, p // 2, 2],
         PANEL // BLOCK, 0, row_owner, col_owner, s_top, corner_h,
     )
     eye = lax.broadcasted_iota(jnp.int32, (STEP, STEP), 0) == lax.broadcasted_iota(
@@ -137,9 +137,9 @@
 def band_kernel(place, row_owner, col_owner, tiles, inv, factor, high, low, s_buf, h_buf):
     step = pl.program_id(0)
     here = place[0]
-    slot = pl.multiple_of((step // 2) * BLOCK, BLOCK)
+    slot = step // 2
     fetch_panel(
-        lambda i, p, q: tiles[2 * q + p % 2, p // 2, pl.ds(slot, BLOCK), :],
+        lambda i, p, q: tiles[2 * q + p % 2, p // 2, slot],
         PANEL // BLOCK, here * 32 + step * 8, row_owner, col_owner, s_buf, h_buf,
     )
     special = jnp.logical_and(here == 0, step == 0)
@@ -156,7 +156,7 @@
     update = update + dot(ll[...], rh[...], 1, 1)
     out[...] = update
     low = lower_half((BLOCK, 2 * BLOCK))
-    slot = pl.multiple_of((step * blocks // 16) * BLOCK, BLOCK)
+    slot = pl.multiple_of(step * blocks // 16 * BLOCK, BLOCK)
     for i in range(blocks):
         p = row_owner[place[0] * 32 + step * blocks + i]
         for j in range(0, 16, 2):
@@ -170,6 +170,192 @@
             out[at] = both - out[at]
 
 
+def axis_split(r, c):
+    return r // 2, r % 2, c // 8, (c // 2) % 4, c % 2
+
+
+def exchange_kernel(panels, h_ref, zs, xs, outgoing, h_buf, load_sem, store_sem, own_sem,
+                    p1s, p1z, p1t, p1x, sends, gets, sib_s, sib_r):
+    r, c = lax.axis_index("row"), lax.axis_index("col")
+    x, yl, yh, z, core = axis_split(r, c)
+    half_r, half_c = zs.shape[1] // 2, xs.shape[1] // 2
+
+    def col_of(yh_, z_, core_):
+        return yh_ * 8 + (z_ % 4) * 2 + core_
+
+    def row_of(x_, yl_):
+        return (x_ % 4) * 2 + yl_
+
+    barrier = pltpu.get_barrier_semaphore()
+    for d in range(1, 8):
+        pl.semaphore_signal(barrier, inc=1, device_id=((r + d) % 8, c), device_id_type=pl.DeviceIdType.MESH)
+    for d in range(1, 16):
+        pl.semaphore_signal(barrier, inc=1, device_id=(r, (c + d) % 16), device_id_type=pl.DeviceIdType.MESH)
+    loads = []
+    for i in range(8):
+        rows = pl.ds(i * 128, 128)
+        loads.append(pltpu.make_async_copy(h_ref.at[rows], h_buf.at[rows], load_sem.at[i]))
+        loads[-1].start()
+    pl.semaphore_wait(barrier, 22)
+
+    def send(src, dst, ss, rs, to):
+        copy = pltpu.make_async_remote_copy(
+            src_ref=src, dst_ref=dst, send_sem=ss, recv_sem=rs, device_id=to,
+            device_id_type=pl.DeviceIdType.MESH,
+        )
+        copy.start()
+        return copy
+
+    def arrived(ref, sem):
+        pltpu.make_async_copy(ref, ref, sem).wait()
+
+    open_sends = []
+    for d in range(1, 8):
+        to = (r + d) % 8
+        open_sends.append(send(panels.at[0], zs.at[c, r, 2], p1s.at[0, d], p1z.at[d], (to, c)))
+        open_sends.append(
+            send(panels.at[pl.ds(2 * to, 2)], zs.at[c, r, pl.ds(0, 2)], p1s.at[1, d], p1z.at[d], (to, c))
+        )
+    for d in range(1, 16):
+        to = (c + d) % 16
+        open_sends.append(send(panels.at[to], xs.at[r, c], p1t.at[d], p1x.at[d], (r, to)))
+    own = [
+        pltpu.make_async_copy(panels.at[0], zs.at[c, r, 2], own_sem.at[0]),
+        pltpu.make_async_copy(panels.at[pl.ds(2 * r, 2)], zs.at[c, r, pl.ds(0, 2)], own_sem.at[1]),
+        pltpu.make_async_copy(panels.at[c], xs.at[r, c], own_sem.at[2]),
+    ]
+    for copy in own:
+        copy.start()
+
+    zp, zm = (r, col_of(yh, z + 1, core)), (r, col_of(yh, z + 3, core))
+    yp, sib = (r, col_of(1 - yh, z, core)), (r, col_of(yh, z, 1 - core))
+    xp, xm, lp = (row_of(x + 1, yl), c), (row_of(x + 3, yl), c), (row_of(x, 1 - yl), c)
+
+    def chunk_z(k):
+        return zs.at[k]
+
+    def chunk_x(k):
+        return xs.at[k]
+
+    def first(ref, k):
+        return ref.at[k, pl.ds(0, ref.shape[1] // 2)]
+
+    def second(ref, k):
+        return ref.at[k, pl.ds(ref.shape[1] // 2, ref.shape[1] // 2)]
+
+    def out(ref, i, to):
+        open_sends.append(send(ref, ref, sends.at[i], gets.at[i], to))
+
+    def share(k, i):
+        open_sends.append(send(zs.at[k], zs.at[k], sib_s.at[i], sib_r.at[i], sib))
+
+    own[0].wait()
+    own[1].wait()
+    for d in range(1, 8):
+        arrived(zs.at[c, (r + 8 - d) % 8], p1z.at[d])
+    out(chunk_z(c), 0, yp)
+    out(chunk_z(c), 1, zp)
+    out(chunk_z(c), 2, zm)
+    own[2].wait()
+    for d in range(1, 16):
+        arrived(xs.at[r, (c + 16 - d) % 16], p1x.at[d])
+    out(chunk_x(r), 3, lp)
+    out(chunk_x(r), 4, xp)
+    out(chunk_x(r), 5, xm)
+    share(c, 0)
+
+    for i in range(8):
+        loads[i].wait()
+
+    def tile(n, carry):
+        i, j = n // 16, n % 16
+        columns = pl.ds(pl.multiple_of(j * 128, 128), 128)
+        rows = pl.ds(pl.multiple_of(i * 128, 128), 128)
+        pltpu.make_async_copy(h_buf.at[rows, columns], outgoing.at[i, j], store_sem).start()
+        return carry
+
+    lax.fori_loop(0, 128, tile, 0)
+
+    def c_at(yh_, dz):
+        return col_of(yh_, z + dz, core)
+
+    arrived(chunk_x(row_of(x + 3, yl)), gets.at[4])
+    out(first(xs, row_of(x + 3, yl)), 6, xp)
+    arrived(chunk_x(row_of(x + 1, yl)), gets.at[5])
+    out(second(xs, row_of(x + 1, yl)), 7, xm)
+    arrived(chunk_x(row_of(x, 1 - yl)), gets.at[3])
+    out(chunk_x(row_of(x, 1 - yl)), 8, xp)
+    out(chunk_x(row_of(x, 1 - yl)), 9, xm)
+
+    arrived(chunk_z(c_at(yh, 3)), gets.at[1])
+    out(first(zs, c_at(yh, 3)), 10, zp)
+    arrived(chunk_z(c_at(yh, 1)), gets.at[2])
+    out(second(zs, c_at(yh, 1)), 11, zm)
+    arrived(chunk_z(c_at(1 - yh, 0)), gets.at[0])
+    out(chunk_z(c_at(1 - yh, 0)), 12, zp)
+    out(chunk_z(c_at(1 - yh, 0)), 13, zm)
+    share(c_at(yh, 3), 1)
+    share(c_at(yh, 1), 2)
+    share(c_at(1 - yh, 0), 3)
+
+    arrived(chunk_x(row_of(x + 3, 1 - yl)), gets.at[8])
+    out(first(xs, row_of(x + 3, 1 - yl)), 14, xp)
+    arrived(chunk_x(row_of(x + 1, 1 - yl)), gets.at[9])
+    out(second(xs, row_of(x + 1, 1 - yl)), 15, xm)
+
+    arrived(first(zs, c_at(yh, 2)), gets.at[10])
+    arrived(second(zs, c_at(yh, 2)), gets.at[11])
+    share(c_at(yh, 2), 4)
+    arrived(chunk_z(c_at(1 - yh, 3)), gets.at[12])
+    out(first(zs, c_at(1 - yh, 3)), 16, zp)
+    arrived(chunk_z(c_at(1 - yh, 1)), gets.at[13])
+    out(second(zs, c_at(1 - yh, 1)), 17, zm)
+    share(c_at(1 - yh, 3), 5)
+    share(c_at(1 - yh, 1), 6)
+
+    arrived(first(xs, row_of(x + 2, yl)), gets.at[6])
+    arrived(second(xs, row_of(x + 2, yl)), gets.at[7])
+    arrived(first(xs, row_of(x + 2, 1 - yl)), gets.at[14])
+    arrived(second(xs, row_of(x + 2, 1 - yl)), gets.at[15])
+    arrived(first(zs, c_at(1 - yh, 2)), gets.at[16])
+    arrived(second(zs, c_at(1 - yh, 2)), gets.at[17])
+    share(c_at(1 - yh, 2), 7)
+
+    def theirs(yh_, dz):
+        return zs.at[col_of(yh_, z + dz, 1 - core)]
+
+    order = [(yh, 0), (yh, 3), (yh, 1), (1 - yh, 0), (yh, 2), (1 - yh, 3), (1 - yh, 1), (1 - yh, 2)]
+    for i, (yh_, dz) in enumerate(order):
+        arrived(theirs(yh_, dz), sib_r.at[i])
+    arrived(outgoing, store_sem)
+    for copy in open_sends:
+        copy.wait_send()
+
+
+def exchange(panels, local_h):
+    any_space = pl.BlockSpec(memory_space=pl.ANY)
+    dma = pltpu.SemaphoreType.DMA
+    return pl.pallas_call(
+        exchange_kernel,
+        out_shape=(
+            shape_of((16, 8, 3, BLOCK, 128)),
+            shape_of((8, 16, BLOCK, 128)),
+            shape_of((8, 16, 128, 128)),
+        ),
+        in_specs=[pl.BlockSpec(memory_space=pltpu.VMEM), any_space],
+        out_specs=(any_space,) * 3,
+        scratch_shapes=[
+            pltpu.VMEM(local_h.shape, F32), dma((8,)), dma, dma((3,)),
+            dma((2, 8)), dma((8,)), dma((16,)), dma((16,)), dma((18,)), dma((18,)), dma((8,)), dma((8,)),
+        ],
+        compiler_params=pltpu.CompilerParams(
+            collective_id=0, has_side_effects=True, vmem_limit_bytes=60 * 2**20
+        ),
+        cost_estimate=pl.CostEstimate(flops=0, bytes_accessed=64 * 2**20, transcendentals=0),
+        name="exchange",
+    )(panels, local_h)
+
+
 def whole(shape):
     return pl.BlockSpec(shape, lambda *i: (0,) * len(shape), pipeline_mode=pl.Buffered(1))
 
@@ -193,9 +379,11 @@
     band = ORDER // rows_n
     strip = ORDER // cols_n
     panels = jnp.concatenate([local_s, local_h[:, :BLOCK]], axis=1)
-
-    top = lax.all_gather(panels[:BLOCK], "row", axis=0)
-    top = lax.all_gather(top, "col", axis=0)
+    band_tiles, strip_tiles, outgoing = exchange(panels.reshape(16, BLOCK, 128), local_h)
+    h_tiles = lax.all_to_all(
+        outgoing.reshape(rows_n * cols_n, 128, 128), ("row", "col"), 0, 0, tiled=True
+    ).reshape(rows_n, cols_n, 128, 128)
+
     inverse, corner_h = pl.pallas_call(
         corner_kernel,
         out_shape=(shape_of((PANEL, PANEL)), shape_of((PANEL, PANEL))),
@@ -209,17 +397,7 @@
         compiler_params=LIMIT,
         cost_estimate=pl.CostEstimate(flops=3 * 10**10, bytes_accessed=6 * 2**20, transcendentals=0),
         name="corner",
-    )(row_owner, col_owner, top)
-
-    band_tiles = lax.all_to_all(panels.reshape(rows_n, 128, 128), "row", 0, 0, tiled=True)
-    band_tiles = lax.all_gather(band_tiles, "col", axis=0)
-    strip_tiles = lax.all_to_all(panels.reshape(cols_n, BLOCK, 128), "col", 0, 0, tiled=True)
-    strip_tiles = lax.all_gather(strip_tiles, "row", axis=0)
-
-    outgoing = local_h.reshape(rows_n, 128, cols_n, 128).transpose(0, 2, 1, 3)
-    h_tiles = lax.all_to_all(
-        outgoing.reshape(rows_n * cols_n, 128, 128), ("row", "col"), 0, 0, tiled=True
-    ).reshape(rows_n, cols_n, 128, 128)
+    )(row_owner, col_owner, band_tiles)
 
     buffers = [pltpu.VMEM((PANEL, PANEL), F32), pltpu.VMEM((PANEL, PANEL), F32)]
     right_high, right_low = pl.pallas_call(

time: 394 us -> 232 us (0.59)
  waiting for transfers between devices: 210 us -> 36.3 us
  Pallas kernels: 81.9 us -> 178 us
  blocking collectives: 63.2 us -> 0 us
  between operations: 13.8 us -> 0.66 us
  local copies, waits for them, and re-layouts: 14.5 us -> 2.22 us
    all_gather x3 -> x0, waiting for transfers between devices: 210 us -> none  [the longest x1 142 us: per_device(): strip_tiles = lax.all_gather(strip_tiles, 'row', axis=0)]
    pallas_call x0 -> x1, Pallas kernels: none -> 92.8 us  [exchange(): pl.pallas_call(exchange_kernel, out_shape=(shape_of((16, 8, 3, BLOCK, 128...]
    all_to_all x2 -> x0, blocking collectives: 38.2 us -> none  [the longest x1 27.5 us: per_device(): lax.all_to_all(panels.reshape(cols_n, BLOCK, 128), 'col', 0, 0, tiled=True)]
    all_to_all x1, waiting for transfers between devices: 0.01 us -> 36.3 us  [per_device(): lax.all_to_all(outgoing.reshape(rows_n * cols_n, 128, 128), ('row', 'col'...]
    all_gather x1 -> x0, blocking collectives: 25 us -> none  [per_device(): top = lax.all_gather(panels[:BLOCK], 'row', axis=0)]
    transpose x2 -> x0, local copies, waits for them, and re-layouts: 6.44 us -> none  [per_device(): outgoing = local_h.reshape(rows_n, 128, cols_n, 128).transpose(0, 2, 1, 3)]
    unnamed x2 -> x1, local copies, waits for them, and re-layouts: 6.95 us -> 1.15 us
  transfers between devices with their start and end apart: 4 -> 1, of which waited for: 3 -> 1; matrix products, arithmetic and copies ran while one was open for 3% -> 0% of each run, Pallas kernels for 15% -> 28%
where the time goes in v2:
time: 232 us; the launch traced here: 228 us
  Pallas kernels  178 us (77%)
  waiting for transfers between devices  36.3 us (16%)
  starting transfers between devices  9.09 us (4%)
    pallas_call x1, Pallas kernels, exchange(): pl.pallas_call(exchange_kernel, out_shape=(shape_of((16, 8, 3, BLOCK, 128...  92.8 us
    all_to_all x1, waiting for transfers between devices, per_device(): lax.all_to_all(outgoing.reshape(rows_n * cols_n, 128, 128), ('row', 'col'...  36.3 us
    pallas_call x1, Pallas kernels, per_device(): pl.pallas_call(corner_kernel, out_shape=(shape_of((PANEL, PANEL)), shape_...  28.2 us
    pallas_call x1, Pallas kernels, per_device(): pl.pallas_call(band_kernel, grid=(band // PANEL,), out_shape=(shape_of((b...  21.3 us
    pallas_call x1, Pallas kernels, per_device(): pl.pallas_call(final_kernel, grid=(band // tall,), out_shape=shape_of((ba...  20.9 us
    pallas_call x1, Pallas kernels, per_device(): pl.pallas_call(strip_kernel, grid=(strip // PANEL,), out_shape=(shape_of(...  15.2 us
    all_to_all x1, starting transfers between devices, per_device(): lax.all_to_all(outgoing.reshape(rows_n * cols_n, 128, 128), ('row', 'col'...  9.09 us
  transfers between devices with their start and end apart: 1, of which 1 were waited for; matrix products, arithmetic and copies ran while one was open for 0% of the time, Pallas kernels for 28%

profile of v2, /device:TPU:1, one launch (start us, length us, event | category | flops | bytes accessed | tf_op | source)
XLA Modules:
  0.0 228.3 jit_solution(8202678107308677984)
XLA Ops:
  0.6 1.1 slice.4
  1.7 1.1 copy.6
  2.9 1.0 pad_maximum_fusion.panels
  3.9 92.8 %exchange.1 = (f32[16,8,3,64,128]{4,3,2,1,0:T(8,128)}, f32[8,16,64,128]{3,2,1,0:T(8,128)}, f32[8,16,128,128]{3,2,1,0:T(8,128)}) custom-call(f32[16,64,128]{2,1,0:T(8,128)} %pad_maximum_fusion.panels, f32[1024,2048]{1,0:T(8,128)} %bitcast.8), custom_call_target="tpu_custom_call" | custom-call | bytes 67108864 | tf_op jit(solution)/shard_map/exchange/pallas_call | solution.py:338
  96.6 9.1 %all-to-all-start = ((f32[128,128,128]{2,1,0:T(8,128)}), f32[128,128,128]{2,1,0:T(8,128)}, u32[]{:S(2)}, u32[]{:S(2)}) async-start(f32[128,128,128]{2,1,0:T(8,128)} %bitcast.9), calls=%async_computation | async-start | bytes 16777216 | tf_op jit(solution)/shard_map/all_to_all | solution.py:383
  105.7 0.6 pad_add_fusion.place
  106.4 28.2 %corner.1 = (f32[512,512]{1,0:T(8,128)}, f32[512,512]{1,0:T(8,128)}) custom-call(s32[256]{0:T(256)} %row_owner.7, s32[256]{0:T(256)} %col_owner.7, f32[16,8,3,64,128]{4,3,2,1,0:T(8,128)} %get-tuple-element.13.tiles), custom_call_target="tpu_custom_call" | custom-call | flops 30000001024 | bytes 6291456 | tf_op jit(solution)/shard_map/corner/pallas_call | solution.py:387
  134.6 15.2 %strip.1 = (bf16[1024,1024]{1,0:T(8,128)(2,1)}, bf16[1024,1024]{1,0:T(8,128)(2,1)}) custom-call(s32[2]{0:T(128)} %pad_add_fusion.place, s32[256]{0:T(256)} %row_owner.7, s32[256]{0:T(256)} %col_owner.7, f32[8,16,64,128]{3,2,1,0:T(8,128)} %get-tuple-element.17.tiles, f32[512,512]{1,0:T(8,128)} %get-tuple-element.14.inv, f32[512,512]{1,0:T(8,128)} %get-tuple-element.18.corner_h), custom_call_target="tpu_custom_call" | custom-call | flops 10000000000 | bytes 10485760 | tf_op jit(solution)/shard_map/strip/pallas_call | solution.py:403
  149.8 21.3 %band.1 = (f32[2048,512]{1,0:T(8,128)}, bf16[2048,1024]{1,0:T(8,128)(2,1)}, bf16[2048,1024]{1,0:T(8,128)(2,1)}) custom-call(s32[2]{0:T(128)} %pad_add_fusion.place, s32[256]{0:T(256)} %row_owner.7, s32[256]{0:T(256)} %col_owner.7, f32[16,8,3,64,128]{4,3,2,1,0:T(8,128)} %get-tuple-element.13.tiles, f32[512,512]{1,0:T(8,128)} %get-tuple-element.14.inv), custom_call_target="tpu_custom_call" | custom-call | flops 12999999488 | bytes 20971520 | tf_op jit(solution)/shard_map/band/pallas_call | solution.py:415
  171.1 36.3 %all-to-all-done = f32[128,128,128]{2,1,0:T(8,128)} async-done(((f32[128,128,128]{2,1,0:T(8,128)}), f32[128,128,128]{2,1,0:T(8,128)}, u32[]{:S(2)}, u32[]{:S(2)}) %all-to-all-start) | async-done | bytes 8388640 | tf_op jit(solution)/shard_map/all_to_all | solution.py:383
  207.4 20.9 %final.1 = f32[2048,1024]{1,0:T(8,128)} custom-call(s32[2]{0:T(128)} %pad_add_fusion.place, s32[256]{0:T(256)} %row_owner.7, s32[256]{0:T(256)} %col_owner.7, f32[8,16,128,128]{3,2,1,0:T(8,128)} %bitcast.6.tiles, bf16[2048,1024]{1,0:T(8,128)(2,1)} %get-tuple-element.15.lh, bf16[2048,1024]{1,0:T(8,128)(2,1)} %get-tuple-element.16.ll, ...), custom_call_target="tpu_custom_call" | custom-call | flops 12999999488 | bytes 29360128 | tf_op jit(solution)/shard_map/final/pallas_call | solution.py:429
Async XLA Ops:
  96.6 110.8 %all-to-all-start = ((f32[128,128,128]{2,1,0:T(8,128)}), f32[128,128,128]{2,1,0:T(8,128)}, u32[]{:S(2)}, u32[]{:S(2)}) async-start(f32[128,128,128]{2,1,0:T(8,128)} %bitcast.9), calls=%async_computation | async-start | bytes 16777216 | tf_op jit(solution)/shard_map/all_to_all | solution.py:383

commit v3 on v2

--- a/solution.py
+++ b/solution.py
@@ -1,3 +1,5 @@
+import functools
+
 import jax
 import jax.numpy as jnp
 from jax import lax
@@ -82,7 +84,7 @@
 
 def corner_kernel(row_owner, col_owner, tiles, inverse, corner_h, s_top, work, a_blk, b_blk):
     fetch_panel(
-        lambda i, p, q: tiles[2 * q + p % 2, p // 2, 2],
+        lambda i, p, q: tiles[2 * q + p % 2, p // 2, 0],
         PANEL // BLOCK, 0, row_owner, col_owner, s_top, corner_h,
     )
     eye = lax.broadcasted_iota(jnp.int32, (STEP, STEP), 0) == lax.broadcasted_iota(
@@ -137,9 +139,8 @@
 def band_kernel(place, row_owner, col_owner, tiles, inv, factor, high, low, s_buf, h_buf):
     step = pl.program_id(0)
     here = place[0]
-    slot = step // 2
     fetch_panel(
-        lambda i, p, q: tiles[2 * q + p % 2, p // 2, slot],
+        lambda i, p, q: tiles[2 * q + p % 2, p // 2, 0],
         PANEL // BLOCK, here * 32 + step * 8, row_owner, col_owner, s_buf, h_buf,
     )
     special = jnp.logical_and(here == 0, step == 0)
@@ -148,7 +149,8 @@
     high[:, PANEL:], low[:, PANEL:] = halves(h_buf[...])
 
 
-def final_kernel(place, row_owner, col_owner, tiles, lh, ll, rh, rl, out):
+def final_kernel(part, place, row_owner, col_owner, tiles, lh, ll, rh, rl, *refs):
+    out = refs[-1]
     step = pl.program_id(0)
     blocks = out.shape[0] // BLOCK
     update = dot(lh[...], rh[...], 1, 1)
@@ -156,12 +158,11 @@
     update = update + dot(ll[...], rh[...], 1, 1)
     out[...] = update
     low = lower_half((BLOCK, 2 * BLOCK))
-    slot = pl.multiple_of(step * blocks // 16 * BLOCK, BLOCK)
     for i in range(blocks):
-        p = row_owner[place[0] * 32 + step * blocks + i]
+        p = row_owner[place[0] * 32 + part * 16 + step * blocks + i]
         for j in range(0, 16, 2):
-            one = tiles[p // 2, 2 * col_owner[place[1] * 16 + j] + p % 2, pl.ds(slot, BLOCK), :]
-            two = tiles[p // 2, 2 * col_owner[place[1] * 16 + j + 1] + p % 2, pl.ds(slot, BLOCK), :]
+            one = tiles[p // 2, 2 * col_owner[place[1] * 16 + j] + p % 2]
+            two = tiles[p // 2, 2 * col_owner[place[1] * 16 + j + 1] + p % 2]
             if j < 8:
                 both = jnp.where(low, one, pltpu.roll(two, BLOCK, 1))
             else:
@@ -174,8 +175,8 @@
     return r // 2, r % 2, c // 8, (c // 2) % 4, c % 2
 
 
-def exchange_kernel(panels, h_ref, zs, xs, outgoing, h_buf, load_sem, store_sem, own_sem,
-                    p1s, p1z, p1t, p1x, sends, gets, sib_s, sib_r):
+def exchange_kernel(panels, h_ref, zs, xs, near, outgoing, h_buf, load_sem, store_sem, own_sem,
+                    p1s, p1z, p1t, p1x, sends, gets, sib_s, sib_r, h_sent, h_got):
     r, c = lax.axis_index("row"), lax.axis_index("col")
     x, yl, yh, z, core = axis_split(r, c)
     half_r, half_c = zs.shape[1] // 2, xs.shape[1] // 2
@@ -186,17 +187,11 @@
     def row_of(x_, yl_):
         return (x_ % 4) * 2 + yl_
 
-    barrier = pltpu.get_barrier_semaphore()
-    for d in range(1, 8):
-        pl.semaphore_signal(barrier, inc=1, device_id=((r + d) % 8, c), device_id_type=pl.DeviceIdType.MESH)
-    for d in range(1, 16):
-        pl.semaphore_signal(barrier, inc=1, device_id=(r, (c + d) % 16), device_id_type=pl.DeviceIdType.MESH)
     loads = []
     for i in range(8):
         rows = pl.ds(i * 128, 128)
         loads.append(pltpu.make_async_copy(h_ref.at[rows], h_buf.at[rows], load_sem.at[i]))
         loads[-1].start()
-    pl.semaphore_wait(barrier, 22)
 
     def send(src, dst, ss, rs, to):
         copy = pltpu.make_async_remote_copy(
@@ -227,6 +222,34 @@
     for copy in own:
         copy.start()
 
+    for i in range(8):
+        loads[i].wait()
+
+    def upper(i, j):
+        rows = pl.ds(pl.multiple_of(i * 128, 128), BLOCK)
+        return h_buf.at[rows, pl.ds(pl.multiple_of(j * 128, 128), 128)]
+
+    def send_tile(n, carry):
+        i, j = (r + n % 8) % 8, (c + n // 8) % 16
+        pltpu.make_async_remote_copy(
+            src_ref=upper(i, j), dst_ref=near.at[r * 16 + c], send_sem=h_sent, recv_sem=h_got,
+            device_id=(i, j), device_id_type=pl.DeviceIdType.MESH,
+        ).start()
+        return carry
+
+    def batch(n):
+        lax.fori_loop(max(16 * n, 1), 16 * n + 16, send_tile, 0)
+
+    def store_tile(n, carry):
+        i, j = n // 16, n % 16
+        rows = pl.ds(pl.multiple_of(i * 128 + BLOCK, BLOCK), BLOCK)
+        columns = pl.ds(pl.multiple_of(j * 128, 128), 128)
+        pltpu.make_async_copy(h_buf.at[rows, columns], outgoing.at[i, j], store_sem).start()
+        return carry
+
+    batch(0)
+    pltpu.make_async_copy(upper(r, c), near.at[r * 16 + c], h_got).start()
+
     zp, zm = (r, col_of(yh, z + 1, core)), (r, col_of(yh, z + 3, core))
     yp, sib = (r, col_of(1 - yh, z, core)), (r, col_of(yh, z, 1 - core))
     xp, xm, lp = (row_of(x + 1, yl), c), (row_of(x + 3, yl), c), (row_of(x, 1 - yl), c)
@@ -263,18 +286,8 @@
     out(chunk_x(r), 4, xp)
     out(chunk_x(r), 5, xm)
     share(c, 0)
-
-    for i in range(8):
-        loads[i].wait()
-
-    def tile(n, carry):
-        i, j = n // 16, n % 16
-        columns = pl.ds(pl.multiple_of(j * 128, 128), 128)
-        rows = pl.ds(pl.multiple_of(i * 128, 128), 128)
-        pltpu.make_async_copy(h_buf.at[rows, columns], outgoing.at[i, j], store_sem).start()
-        return carry
-
-    lax.fori_loop(0, 128, tile, 0)
+    lax.fori_loop(0, 128, store_tile, 0)
+    batch(1)
 
     def c_at(yh_, dz):
         return col_of(yh_, z + dz, core)
@@ -283,17 +296,21 @@
     out(first(xs, row_of(x + 3, yl)), 6, xp)
     arrived(chunk_x(row_of(x + 1, yl)), gets.at[5])
     out(second(xs, row_of(x + 1, yl)), 7, xm)
+    batch(2)
     arrived(chunk_x(row_of(x, 1 - yl)), gets.at[3])
     out(chunk_x(row_of(x, 1 - yl)), 8, xp)
     out(chunk_x(row_of(x, 1 - yl)), 9, xm)
+    batch(3)
 
     arrived(chunk_z(c_at(yh, 3)), gets.at[1])
     out(first(zs, c_at(yh, 3)), 10, zp)
     arrived(chunk_z(c_at(yh, 1)), gets.at[2])
     out(second(zs, c_at(yh, 1)), 11, zm)
+    batch(4)
     arrived(chunk_z(c_at(1 - yh, 0)), gets.at[0])
     out(chunk_z(c_at(1 - yh, 0)), 12, zp)
     out(chunk_z(c_at(1 - yh, 0)), 13, zm)
+    batch(5)
     share(c_at(yh, 3), 1)
     share(c_at(yh, 1), 2)
     share(c_at(1 - yh, 0), 3)
@@ -302,6 +319,7 @@
     out(first(xs, row_of(x + 3, 1 - yl)), 14, xp)
     arrived(chunk_x(row_of(x + 1, 1 - yl)), gets.at[9])
     out(second(xs, row_of(x + 1, 1 - yl)), 15, xm)
+    batch(6)
 
     arrived(first(zs, c_at(yh, 2)), gets.at[10])
     arrived(second(zs, c_at(yh, 2)), gets.at[11])
@@ -310,6 +328,7 @@
     out(first(zs, c_at(1 - yh, 3)), 16, zp)
     arrived(chunk_z(c_at(1 - yh, 1)), gets.at[13])
     out(second(zs, c_at(1 - yh, 1)), 17, zm)
+    batch(7)
     share(c_at(1 - yh, 3), 5)
     share(c_at(1 - yh, 1), 6)
 
@@ -328,6 +347,8 @@
     for i, (yh_, dz) in enumerate(order):
         arrived(theirs(yh_, dz), sib_r.at[i])
     arrived(outgoing, store_sem)
+    arrived(near, h_got)
+    arrived(near.at[pl.ds(0, 127)], h_sent)
     for copy in open_sends:
         copy.wait_send()
 
@@ -340,16 +361,18 @@
         out_shape=(
             shape_of((16, 8, 3, BLOCK, 128)),
             shape_of((8, 16, BLOCK, 128)),
-            shape_of((8, 16, 128, 128)),
+            shape_of((128, BLOCK, 128)),
+            shape_of((8, 16, BLOCK, 128)),
         ),
         in_specs=[pl.BlockSpec(memory_space=pltpu.VMEM), any_space],
-        out_specs=(any_space,) * 3,
+        out_specs=(any_space,) * 4,
         scratch_shapes=[
             pltpu.VMEM(local_h.shape, F32), dma((8,)), dma, dma((3,)),
             dma((2, 8)), dma((8,)), dma((16,)), dma((16,)), dma((18,)), dma((18,)), dma((8,)), dma((8,)),
+            dma, dma,
         ],
         compiler_params=pltpu.CompilerParams(
-            collective_id=0, has_side_effects=True, vmem_limit_bytes=60 * 2**20
+            has_side_effects=True, vmem_limit_bytes=60 * 2**20
         ),
         cost_estimate=pl.CostEstimate(flops=0, bytes_accessed=64 * 2**20, transcendentals=0),
         name="exchange",
@@ -379,15 +402,18 @@
     band = ORDER // rows_n
     strip = ORDER // cols_n
     panels = jnp.concatenate([local_s, local_h[:, :BLOCK]], axis=1)
-    band_tiles, strip_tiles, outgoing = exchange(panels.reshape(16, BLOCK, 128), local_h)
-    h_tiles = lax.all_to_all(
-        outgoing.reshape(rows_n * cols_n, 128, 128), ("row", "col"), 0, 0, tiled=True
-    ).reshape(rows_n, cols_n, 128, 128)
+    band_tiles, strip_tiles, near, outgoing = exchange(panels.reshape(16, BLOCK, 128), local_h)
+    far = lax.all_to_all(
+        outgoing.reshape(rows_n * cols_n, BLOCK, 128), ("row", "col"), 0, 0, tiled=True
+    )
+    h_parts = [part.reshape(rows_n, cols_n, BLOCK, 128) for part in (near, far)]
 
     inverse, corner_h = pl.pallas_call(
         corner_kernel,
         out_shape=(shape_of((PANEL, PANEL)), shape_of((PANEL, PANEL))),
-        in_specs=[SMEM, SMEM, pl.BlockSpec(memory_space=pltpu.VMEM)],
+        grid=(1,),
+        in_specs=[SMEM, SMEM, pl.BlockSpec((16, 8, 1, BLOCK, 128), lambda i: (0, 0, 2, 0, 0))],
+        out_specs=(whole((PANEL, PANEL)),) * 2,
         scratch_shapes=[
             pltpu.VMEM((PANEL, PANEL), F32),
             pltpu.VMEM((PANEL // STEP, STEP, 2 * PANEL), F32),
@@ -416,7 +442,7 @@
         band_kernel,
         grid=(band // PANEL,),
         out_shape=(shape_of((band, PANEL)),) + (shape_of((band, 2 * PANEL), BF16),) * 2,
-        in_specs=[SMEM, SMEM, SMEM, whole(band_tiles.shape), whole((PANEL, PANEL))],
+        in_specs=[SMEM, SMEM, SMEM, pl.BlockSpec((16, 8, 1, BLOCK, 128), lambda i: (0, 0, i // 2, 0, 0)), whole((PANEL, PANEL))],
         out_specs=(pl.BlockSpec((PANEL, PANEL), lambda i: (i, 0)),)
         + (pl.BlockSpec((PANEL, 2 * PANEL), lambda i: (i, 0)),) * 2,
         scratch_shapes=buffers,
@@ -426,18 +452,27 @@
     )(place, row_owner, col_owner, band_tiles, inverse)
 
     tall = 256
-    h_block = pl.pallas_call(
-        final_kernel,
-        grid=(band // tall,),
-        out_shape=shape_of((band, strip)),
-        in_specs=[SMEM, SMEM, SMEM, whole(h_tiles.shape)]
-        + [pl.BlockSpec((tall, 2 * PANEL), lambda i: (i, 0))] * 2
-        + [whole((strip, 2 * PANEL))] * 2,
-        out_specs=pl.BlockSpec((tall, strip), lambda i: (i, 0)),
-        compiler_params=LIMIT,
-        cost_estimate=pl.CostEstimate(flops=13 * 10**9, bytes_accessed=28 * 2**20, transcendentals=0),
-        name="final",
-    )(place, row_owner, col_owner, h_tiles, left_high, left_low, right_high, right_low)
+    count = band // tall // 2
+    h_block = None
+    for part in range(2):
+        row_tile = lambda i, part=part: (i + part * count, 0)
+        before = [] if h_block is None else [h_block]
+        h_block = pl.pallas_call(
+            functools.partial(final_kernel, part),
+            grid=(count,),
+            out_shape=shape_of((band, strip)),
+            in_specs=[SMEM, SMEM, SMEM, whole(h_parts[part].shape)]
+            + [pl.BlockSpec((tall, 2 * PANEL), row_tile)] * 2
+            + [whole((strip, 2 * PANEL))] * 2
+            + [pl.BlockSpec(memory_space=pl.ANY)] * len(before),
+            out_specs=pl.BlockSpec((tall, strip), row_tile),
+            input_output_aliases={8: 0} if before else {},
+            compiler_params=LIMIT,
+            cost_estimate=pl.CostEstimate(
+                flops=65 * 10**8, bytes_accessed=14 * 2**20, transcendentals=0
+            ),
+            name=f"final_{part}",
+        )(place, row_owner, col_owner, h_parts[part], left_high, left_low, right_high, right_low, *before)
     return h_block, factor
 
 

time: 232 us -> 252 us (1.086); the launches traced: 228 us -> 251 us
  Pallas kernels: 178 us -> 227 us
  waiting for transfers between devices: 36.3 us -> 0.01 us
  starting transfers between devices: 9.09 us -> 20.1 us
    pallas_call x1, Pallas kernels: 92.8 us -> 142 us  [exchange(): pl.pallas_call(exchange_kernel, out_shape=(shape_of((16, 8, 3, BLOCK, 128...]
    all_to_all x1, waiting for transfers between devices: 36.3 us -> 0.01 us  [per_device(): lax.all_to_all(outgoing.reshape(rows_n * cols_n, BLOCK, 128), ('row', 'co...]
    all_to_all x1, starting transfers between devices: 9.09 us -> 20.1 us  [per_device(): lax.all_to_all(outgoing.reshape(rows_n * cols_n, BLOCK, 128), ('row', 'co...]
    pallas_call x1 -> x2, Pallas kernels: 20.9 us -> 24.4 us  [per_device(): pl.pallas_call(functools.partial(final_kernel, part), grid=(count,), out_...]
  transfers between devices with their start and end apart: 1 -> 1, of which waited for: 1 -> 0; matrix products, arithmetic and copies ran while one was open for 0% -> 0% of each run, Pallas kernels for 28% -> 29%
where the time goes in v3:
time: 252 us; the launch traced here: 251 us
  Pallas kernels  227 us (90%)
  starting transfers between devices  20.1 us (8%)
    pallas_call x1, Pallas kernels, exchange(): pl.pallas_call(exchange_kernel, out_shape=(shape_of((16, 8, 3, BLOCK, 128...  142 us
    pallas_call x1, Pallas kernels, per_device(): pl.pallas_call(corner_kernel, out_shape=(shape_of((PANEL, PANEL)), shape_...  25.9 us
    pallas_call x2, Pallas kernels, per_device(): pl.pallas_call(functools.partial(final_kernel, part), grid=(count,), out_...  24.4 us
    all_to_all x1, starting transfers between devices, per_device(): lax.all_to_all(outgoing.reshape(rows_n * cols_n, BLOCK, 128), ('row', 'co...  20.1 us
    pallas_call x1, Pallas kernels, per_device(): pl.pallas_call(band_kernel, grid=(band // PANEL,), out_shape=(shape_of((b...  19 us
    pallas_call x1, Pallas kernels, per_device(): pl.pallas_call(strip_kernel, grid=(strip // PANEL,), out_shape=(shape_of(...  15.2 us
  transfers between devices with their start and end apart: 1, of which 0 were waited for; matrix products, arithmetic and copies ran while one was open for 0% of the time, Pallas kernels for 29%

profile of v3, /device:TPU:1, one launch (start us, length us, event | category | flops | bytes accessed | tf_op | source)
XLA Modules:
  0.0 251.5 jit_solution(4503632120209907437)
XLA Ops:
  0.6 1.1 slice.4
  1.7 1.1 copy.7
  2.9 1.0 pad_maximum_fusion.panels
  3.9 142.3 %exchange.1 = (f32[16,8,3,64,128]{4,3,2,1,0:T(8,128)}, f32[8,16,64,128]{3,2,1,0:T(8,128)}, f32[128,64,128]{2,1,0:T(8,128)}, f32[8,16,64,128]{3,2,1,0:T(8,128)}) custom-call(f32[16,64,128]{2,1,0:T(8,128)} %pad_maximum_fusion.panels, f32[1024,2048]{1,0:T(8,128)} %bitcast.9), custom_call_target="tpu_custom_call" | custom-call | bytes 67108864 | tf_op jit(solution)/shard_map/exchange/pallas_call | solution.py:359
  146.2 20.1 %all-to-all-start = ((f32[128,64,128]{2,1,0:T(8,128)}), f32[128,64,128]{2,1,0:T(8,128)}, u32[]{:S(2)}, u32[]{:S(2)}) async-start(f32[128,64,128]{2,1,0:T(8,128)} %bitcast.10), calls=%async_computation | async-start | bytes 8388608 | tf_op jit(solution)/shard_map/all_to_all | solution.py:406
  166.3 25.9 %corner.1 = (f32[512,512]{1,0:T(8,128)}, f32[512,512]{1,0:T(8,128)}) custom-call(s32[256]{0:T(256)} %row_owner.9, s32[256]{0:T(256)} %col_owner.9, f32[16,8,3,64,128]{4,3,2,1,0:T(8,128)} %get-tuple-element.14.tiles), custom_call_target="tpu_custom_call" | custom-call | flops 30000001024 | bytes 6291456 | tf_op jit(solution)/shard_map/corner/pallas_call | solution.py:411
  192.1 0.6 pad_add_fusion.place
  192.8 15.2 %strip.1 = (bf16[1024,1024]{1,0:T(8,128)(2,1)}, bf16[1024,1024]{1,0:T(8,128)(2,1)}) custom-call(s32[2]{0:T(128)} %pad_add_fusion.place, s32[256]{0:T(256)} %row_owner.9, s32[256]{0:T(256)} %col_owner.9, f32[8,16,64,128]{3,2,1,0:T(8,128)} %get-tuple-element.18.tiles, f32[512,512]{1,0:T(8,128)} %get-tuple-element.15.inv, f32[512,512]{1,0:T(8,128)} %get-tuple-element.19.corner_h), custom_call_target="tpu_custom_call" | custom-call | flops 10000000000 | bytes 10485760 | tf_op jit(solution)/shard_map/strip/pallas_call | solution.py:429
  208.0 19.0 %band.1 = (f32[2048,512]{1,0:T(8,128)}, bf16[2048,1024]{1,0:T(8,128)(2,1)}, bf16[2048,1024]{1,0:T(8,128)(2,1)}) custom-call(s32[2]{0:T(128)} %pad_add_fusion.place, s32[256]{0:T(256)} %row_owner.9, s32[256]{0:T(256)} %col_owner.9, f32[16,8,3,64,128]{4,3,2,1,0:T(8,128)} %get-tuple-element.14.tiles, f32[512,512]{1,0:T(8,128)} %get-tuple-element.15.inv), custom_call_target="tpu_custom_call" | custom-call | flops 12999999488 | bytes 20971520 | tf_op jit(solution)/shard_map/band/pallas_call | solution.py:441
  227.0 12.2 %final_0.1.refs_0_ = f32[2048,1024]{1,0:T(8,128)} custom-call(s32[2]{0:T(128)} %pad_add_fusion.place, s32[256]{0:T(256)} %row_owner.9, s32[256]{0:T(256)} %col_owner.9, f32[8,16,64,128]{3,2,1,0:T(8,128)} %bitcast.11, bf16[2048,1024]{1,0:T(8,128)(2,1)} %get-tuple-element.16.lh, bf16[2048,1024]{1,0:T(8,128)(2,1)} %get-tuple-element.17.ll, ...), custom_call_target="tpu_custom_call" | custom-call | flops 6499999744 | bytes 14680064 | tf_op jit(solution)/shard_map/final_0/pallas_call | solution.py:460
  239.3 0.0 all-to-all-done
  239.3 12.2 %final_1.1 = f32[2048,1024]{1,0:T(8,128)} custom-call(s32[2]{0:T(128)} %pad_add_fusion.place, s32[256]{0:T(256)} %row_owner.9, s32[256]{0:T(256)} %col_owner.9, f32[8,16,64,128]{3,2,1,0:T(8,128)} %bitcast.6.tiles, bf16[2048,1024]{1,0:T(8,128)(2,1)} %get-tuple-element.16.lh, bf16[2048,1024]{1,0:T(8,128)(2,1)} %get-tuple-element.17.ll, ...), custom_call_target="tpu_custom_call", output_to_operand_aliasing={{}: (8, {})} | custom-call | flops 6499999744 | bytes 14680064 | tf_op jit(solution)/shard_map/final_1/pallas_call | solution.py:460
Async XLA Ops:
  146.2 93.1 %all-to-all-start = ((f32[128,64,128]{2,1,0:T(8,128)}), f32[128,64,128]{2,1,0:T(8,128)}, u32[]{:S(2)}, u32[]{:S(2)}) async-start(f32[128,64,128]{2,1,0:T(8,128)} %bitcast.10), calls=%async_computation | async-start | bytes 8388608 | tf_op jit(solution)/shard_map/all_to_all | solution.py:406

commit v4 on v2

--- a/solution.py
+++ b/solution.py
@@ -9,6 +9,7 @@
 PANEL = 512
 BLOCK = 64
 STEP = 128
+FINE = 16
 HIGHEST = lax.Precision.HIGHEST
 BF16 = jnp.bfloat16
 F32 = jnp.float32
@@ -82,7 +83,7 @@
 
 def corner_kernel(row_owner, col_owner, tiles, inverse, corner_h, s_top, work, a_blk, b_blk):
     fetch_panel(
-        lambda i, p, q: tiles[2 * q + p % 2, p // 2, 2],
+        lambda i, p, q: tiles[2 * q + p % 2, p // 2, 0],
         PANEL // BLOCK, 0, row_owner, col_owner, s_top, corner_h,
     )
     eye = lax.broadcasted_iota(jnp.int32, (STEP, STEP), 0) == lax.broadcasted_iota(
@@ -137,9 +138,8 @@
 def band_kernel(place, row_owner, col_owner, tiles, inv, factor, high, low, s_buf, h_buf):
     step = pl.program_id(0)
     here = place[0]
-    slot = step // 2
     fetch_panel(
-        lambda i, p, q: tiles[2 * q + p % 2, p // 2, slot],
+        lambda i, p, q: tiles[2 * q + p % 2, p // 2, 0],
         PANEL // BLOCK, here * 32 + step * 8, row_owner, col_owner, s_buf, h_buf,
     )
     special = jnp.logical_and(here == 0, step == 0)
@@ -148,26 +148,27 @@
     high[:, PANEL:], low[:, PANEL:] = halves(h_buf[...])
 
 
-def final_kernel(place, row_owner, col_owner, tiles, lh, ll, rh, rl, out):
-    step = pl.program_id(0)
-    blocks = out.shape[0] // BLOCK
+def update_kernel(lh, ll, rh, rl, out):
     update = dot(lh[...], rh[...], 1, 1)
     update = update + dot(lh[...], rl[...], 1, 1)
-    update = update + dot(ll[...], rh[...], 1, 1)
-    out[...] = update
-    low = lower_half((BLOCK, 2 * BLOCK))
-    slot = pl.multiple_of(step * blocks // 16 * BLOCK, BLOCK)
-    for i in range(blocks):
-        p = row_owner[place[0] * 32 + step * blocks + i]
+    out[...] = update + dot(ll[...], rh[...], 1, 1)
+
+
+def final_kernel(place, row_owner, col_owner, tiles, update, out):
+    slot = pl.program_id(0)
+    low = lower_half((FINE, 2 * BLOCK))
+    owners = [col_owner[place[1] * 16 + j] * 2 for j in range(16)]
+    for i in range(16):
+        p = row_owner[place[0] * 32 + slot * 16 + i]
         for j in range(0, 16, 2):
-            one = tiles[p // 2, 2 * col_owner[place[1] * 16 + j] + p % 2, pl.ds(slot, BLOCK), :]
-            two = tiles[p // 2, 2 * col_owner[place[1] * 16 + j + 1] + p % 2, pl.ds(slot, BLOCK), :]
+            one = tiles[p // 2, owners[j] + p % 2]
+            two = tiles[p // 2, owners[j + 1] + p % 2]
             if j < 8:
                 both = jnp.where(low, one, pltpu.roll(two, BLOCK, 1))
             else:
                 both = jnp.where(low, pltpu.roll(one, BLOCK, 1), two)
-            at = (pl.ds(i * BLOCK, BLOCK), pl.ds(j * BLOCK, 2 * BLOCK))
-            out[at] = both - out[at]
+            at = (i, 0, slice(None), pl.ds(j * BLOCK, 2 * BLOCK))
+            out[at] = both - update[at]
 
 
 def axis_split(r, c):
@@ -387,7 +388,9 @@
     inverse, corner_h = pl.pallas_call(
         corner_kernel,
         out_shape=(shape_of((PANEL, PANEL)), shape_of((PANEL, PANEL))),
-        in_specs=[SMEM, SMEM, pl.BlockSpec(memory_space=pltpu.VMEM)],
+        grid=(1,),
+        in_specs=[SMEM, SMEM, pl.BlockSpec((16, 8, 1, BLOCK, 128), lambda i: (0, 0, 2, 0, 0))],
+        out_specs=(whole((PANEL, PANEL)),) * 2,
         scratch_shapes=[
             pltpu.VMEM((PANEL, PANEL), F32),
             pltpu.VMEM((PANEL // STEP, STEP, 2 * PANEL), F32),
@@ -416,7 +419,7 @@
         band_kernel,
         grid=(band // PANEL,),
         out_shape=(shape_of((band, PANEL)),) + (shape_of((band, 2 * PANEL), BF16),) * 2,
-        in_specs=[SMEM, SMEM, SMEM, whole(band_tiles.shape), whole((PANEL, PANEL))],
+        in_specs=[SMEM, SMEM, SMEM, pl.BlockSpec((16, 8, 1, BLOCK, 128), lambda i: (0, 0, i // 2, 0, 0)), whole((PANEL, PANEL))],
         out_specs=(pl.BlockSpec((PANEL, PANEL), lambda i: (i, 0)),)
         + (pl.BlockSpec((PANEL, 2 * PANEL), lambda i: (i, 0)),) * 2,
         scratch_shapes=buffers,
@@ -426,19 +429,34 @@
     )(place, row_owner, col_owner, band_tiles, inverse)
 
     tall = 256
+    update = pl.pallas_call(
+        update_kernel,
+        grid=(band // tall,),
+        out_shape=shape_of((band, strip)),
+        in_specs=[pl.BlockSpec((tall, 2 * PANEL), lambda i: (i, 0))] * 2
+        + [whole((strip, 2 * PANEL))] * 2,
+        out_specs=pl.BlockSpec((tall, strip), lambda i: (i, 0)),
+        compiler_params=pltpu.CompilerParams(vmem_limit_bytes=60 * 2**20),
+        cost_estimate=pl.CostEstimate(flops=13 * 10**9, bytes_accessed=20 * 2**20, transcendentals=0),
+        name="update",
+    )(left_high, left_low, right_high, right_low)
+
+    fine = pl.BlockSpec((16, 1, FINE, strip), lambda s, u: (s, u, 0, 0))
     h_block = pl.pallas_call(
         final_kernel,
-        grid=(band // tall,),
-        out_shape=shape_of((band, strip)),
-        in_specs=[SMEM, SMEM, SMEM, whole(h_tiles.shape)]
-        + [pl.BlockSpec((tall, 2 * PANEL), lambda i: (i, 0))] * 2
-        + [whole((strip, 2 * PANEL))] * 2,
-        out_specs=pl.BlockSpec((tall, strip), lambda i: (i, 0)),
-        compiler_params=LIMIT,
-        cost_estimate=pl.CostEstimate(flops=13 * 10**9, bytes_accessed=28 * 2**20, transcendentals=0),
+        grid=(2, BLOCK // FINE),
+        out_shape=shape_of((band // BLOCK, BLOCK // FINE, FINE, strip)),
+        in_specs=[
+            SMEM, SMEM, SMEM,
+            pl.BlockSpec((rows_n, cols_n, FINE, 128), lambda s, u: (0, 0, s * (BLOCK // FINE) + u, 0)),
+            fine,
+        ],
+        out_specs=fine,
+        compiler_params=pltpu.CompilerParams(vmem_limit_bytes=60 * 2**20),
+        cost_estimate=pl.CostEstimate(flops=2**22, bytes_accessed=24 * 2**20, transcendentals=0),
         name="final",
-    )(place, row_owner, col_owner, h_tiles, left_high, left_low, right_high, right_low)
-    return h_block, factor
+    )(place, row_owner, col_owner, h_tiles, update.reshape(band // BLOCK, BLOCK // FINE, FINE, strip))
+    return h_block.reshape(band, strip), factor
 
 
 def solution(mesh):

time: 232 us -> 223 us (0.961)
  waiting for transfers between devices: 36.3 us -> 22.6 us
  Pallas kernels: 178 us -> 183 us
    all_to_all x1, waiting for transfers between devices: 36.3 us -> 22.6 us  [per_device(): lax.all_to_all(outgoing.reshape(rows_n * cols_n, 128, 128), ('row', 'col'...]
    pallas_call x1 -> x2, Pallas kernels: 20.9 us -> 30.5 us  [the longest x1 18.3 us: per_device(): pl.pallas_call(update_kernel, grid=(band // tall,), out_shape=shape_of((b...]
    pallas_call x1, Pallas kernels: 28.2 us -> 25.9 us  [per_device(): pl.pallas_call(corner_kernel, out_shape=(shape_of((PANEL, PANEL)), shape_...]
  transfers between devices with their start and end apart: 1 -> 1, of which waited for: 1 -> 1; matrix products, arithmetic and copies ran while one was open for 0% -> 0% of each run, Pallas kernels for 28% -> 36%
where the time goes in v4:
time: 223 us; the launch traced here: 220 us
  Pallas kernels  183 us (82%)
  waiting for transfers between devices  22.6 us (10%)
  starting transfers between devices  9.09 us (4%)
    pallas_call x1, Pallas kernels, exchange(): pl.pallas_call(exchange_kernel, out_shape=(shape_of((16, 8, 3, BLOCK, 128...  92.8 us
    pallas_call x1, Pallas kernels, per_device(): pl.pallas_call(corner_kernel, out_shape=(shape_of((PANEL, PANEL)), shape_...  25.9 us
    all_to_all x1, waiting for transfers between devices, per_device(): lax.all_to_all(outgoing.reshape(rows_n * cols_n, 128, 128), ('row', 'col'...  22.6 us
    pallas_call x1, Pallas kernels, per_device(): pl.pallas_call(band_kernel, grid=(band // PANEL,), out_shape=(shape_of((b...  19 us
    pallas_call x1, Pallas kernels, per_device(): pl.pallas_call(update_kernel, grid=(band // tall,), out_shape=shape_of((b...  18.3 us
    pallas_call x1, Pallas kernels, per_device(): pl.pallas_call(strip_kernel, grid=(strip // PANEL,), out_shape=(shape_of(...  15.3 us
    pallas_call x1, Pallas kernels, per_device(): pl.pallas_call(final_kernel, grid=(2, BLOCK // FINE), out_shape=shape_of(...  12.2 us
    all_to_all x1, starting transfers between devices, per_device(): lax.all_to_all(outgoing.reshape(rows_n * cols_n, 128, 128), ('row', 'col'...  9.09 us
  transfers between devices with their start and end apart: 1, of which 1 were waited for; matrix products, arithmetic and copies ran while one was open for 0% of the time, Pallas kernels for 36%

profile of v4, /device:TPU:1, one launch (start us, length us, event | category | flops | bytes accessed | tf_op | source)
XLA Modules:
  0.0 219.6 jit_solution(9043667897365896019)
XLA Ops:
  0.6 1.1 slice.4
  1.7 1.1 copy.6
  2.9 1.0 pad_maximum_fusion.panels
  3.9 92.8 %exchange.1 = (f32[16,8,3,64,128]{4,3,2,1,0:T(8,128)}, f32[8,16,64,128]{3,2,1,0:T(8,128)}, f32[8,16,128,128]{3,2,1,0:T(8,128)}) custom-call(f32[16,64,128]{2,1,0:T(8,128)} %pad_maximum_fusion.panels, f32[1024,2048]{1,0:T(8,128)} %bitcast.10), custom_call_target="tpu_custom_call" | custom-call | bytes 67108864 | tf_op jit(solution)/shard_map/exchange/pallas_call | solution.py:339
  96.6 9.1 %all-to-all-start = ((f32[128,128,128]{2,1,0:T(8,128)}), f32[128,128,128]{2,1,0:T(8,128)}, u32[]{:S(2)}, u32[]{:S(2)}) async-start(f32[128,128,128]{2,1,0:T(8,128)} %bitcast.11), calls=%async_computation | async-start | bytes 16777216 | tf_op jit(solution)/shard_map/all_to_all | solution.py:384
  105.7 0.6 pad_add_fusion.place
  106.4 25.9 %corner.1 = (f32[512,512]{1,0:T(8,128)}, f32[512,512]{1,0:T(8,128)}) custom-call(s32[256]{0:T(256)} %row_owner.7, s32[256]{0:T(256)} %col_owner.7, f32[16,8,3,64,128]{4,3,2,1,0:T(8,128)} %get-tuple-element.13.tiles), custom_call_target="tpu_custom_call" | custom-call | flops 30000001024 | bytes 6291456 | tf_op jit(solution)/shard_map/corner/pallas_call | solution.py:388
  132.2 15.3 %strip.1 = (bf16[1024,1024]{1,0:T(8,128)(2,1)}, bf16[1024,1024]{1,0:T(8,128)(2,1)}) custom-call(s32[2]{0:T(128)} %pad_add_fusion.place, s32[256]{0:T(256)} %row_owner.7, s32[256]{0:T(256)} %col_owner.7, f32[8,16,64,128]{3,2,1,0:T(8,128)} %get-tuple-element.17.tiles, f32[512,512]{1,0:T(8,128)} %get-tuple-element.14.inv, f32[512,512]{1,0:T(8,128)} %get-tuple-element.18.corner_h), custom_call_target="tpu_custom_call" | custom-call | flops 10000000000 | bytes 10485760 | tf_op jit(solution)/shard_map/strip/pallas_call | solution.py:406
  147.5 19.0 %band.1 = (f32[2048,512]{1,0:T(8,128)}, bf16[2048,1024]{1,0:T(8,128)(2,1)}, bf16[2048,1024]{1,0:T(8,128)(2,1)}) custom-call(s32[2]{0:T(128)} %pad_add_fusion.place, s32[256]{0:T(256)} %row_owner.7, s32[256]{0:T(256)} %col_owner.7, f32[16,8,3,64,128]{4,3,2,1,0:T(8,128)} %get-tuple-element.13.tiles, f32[512,512]{1,0:T(8,128)} %get-tuple-element.14.inv), custom_call_target="tpu_custom_call" | custom-call | flops 12999999488 | bytes 20971520 | tf_op jit(solution)/shard_map/band/pallas_call | solution.py:418
  166.5 18.3 %update.1 = f32[2048,1024]{1,0:T(8,128)} custom-call(bf16[2048,1024]{1,0:T(8,128)(2,1)} %get-tuple-element.15.lh, bf16[2048,1024]{1,0:T(8,128)(2,1)} %get-tuple-element.16.ll, bf16[1024,1024]{1,0:T(8,128)(2,1)} %get-tuple-element.19.rh, bf16[1024,1024]{1,0:T(8,128)(2,1)} %get-tuple-element.20.rl), custom_call_target="tpu_custom_call" | custom-call | flops 12999999488 | bytes 20971520 | tf_op jit(solution)/shard_map/update/pallas_call | solution.py:432
  184.8 22.6 %all-to-all-done = f32[128,128,128]{2,1,0:T(8,128)} async-done(((f32[128,128,128]{2,1,0:T(8,128)}), f32[128,128,128]{2,1,0:T(8,128)}, u32[]{:S(2)}, u32[]{:S(2)}) %all-to-all-start) | async-done | bytes 8388640 | tf_op jit(solution)/shard_map/all_to_all | solution.py:384
  207.4 12.2 %final.1 = f32[32,4,16,1024]{3,2,1,0:T(8,128)} custom-call(s32[2]{0:T(128)} %pad_add_fusion.place, s32[256]{0:T(256)} %row_owner.7, s32[256]{0:T(256)} %col_owner.7, f32[8,16,128,128]{3,2,1,0:T(8,128)} %bitcast.6.tiles, f32[32,4,16,1024]{3,2,1,0:T(8,128)} %bitcast.12), custom_call_target="tpu_custom_call" | custom-call | flops 4194304 | bytes 25165824 | tf_op jit(solution)/shard_map/final/pallas_call | solution.py:445
Async XLA Ops:
  96.6 110.8 %all-to-all-start = ((f32[128,128,128]{2,1,0:T(8,128)}), f32[128,128,128]{2,1,0:T(8,128)}, u32[]{:S(2)}, u32[]{:S(2)}) async-start(f32[128,128,128]{2,1,0:T(8,128)} %bitcast.11), calls=%async_computation | async-start | bytes 16777216 | tf_op jit(solution)/shard_map/all_to_all | solution.py:384

commit v5 on v1

v5 whole, which is shorter than its diff:
```python
import jax
import jax.numpy as jnp
from jax import lax
from jax.experimental import pallas as pl
from jax.experimental.pallas import tpu as pltpu
from jax.sharding import PartitionSpec as P

ORDER = 16384
PANEL = 512
BLOCK = 64
STEP = 128
FINE = 16
TALL = 256
EARLY = 16
HIGHEST = lax.Precision.HIGHEST
BF16 = jnp.bfloat16
F32 = jnp.float32


def dot(a, b, ca, cb, precision=None):
    return lax.dot_general(
        a, b, (((ca,), (cb,)), ((), ())), precision=precision, preferred_element_type=F32
    )


def halves(x):
    high = x.astype(BF16)
    return high, (x - high.astype(F32)).astype(BF16)


def lower_half(shape):
    return lax.broadcasted_iota(jnp.int32, shape, 1) < BLOCK


def fetch_panel(read, rows, first, row_owner, col_owner, s_out, h_out):
    low = lower_half((BLOCK, 2 * BLOCK))
    for i in range(rows):
        p = row_owner[first + i]
        for k in range(0, PANEL // BLOCK, 2):
            one = read(i, p, col_owner[k])
            two = read(i, p, col_owner[k + 1])
            at = (pl.ds(i * BLOCK, BLOCK), pl.ds(k * BLOCK, 2 * BLOCK))
            s_out[at] = jnp.where(low, one, pltpu.roll(two, BLOCK, 1))
            h_out[at] = jnp.where(low, pltpu.roll(one, BLOCK, 1), two)


def spread(x, rows):
    return jnp.broadcast_to(x, (rows, x.shape[1]))


def factor_inverse(a_ref, b_ref):
    sub = lax.broadcasted_iota(jnp.int32, (8, STEP), 0)
    for j in range(0, STEP, 8):
        far = STEP - j - 8
        a_near, b_near = a_ref[j : j + 8, :], b_ref[j : j + 8, :]
        near = [jnp.broadcast_to(a_near[:, j + t : j + t + 1], (8, STEP)) for t in range(8)]
        if far:
            a_far, b_far = a_ref[j + 8 :, :], b_ref[j + 8 :, :]
            cols = [jnp.broadcast_to(a_far[:, j + t : j + t + 1], (far, STEP)) for t in range(8)]
        scales, links = [], []
        for t in range(8):
            r = lax.rsqrt(near[t][t : t + 1, :])
            l = near[t] * spread(r, 8)
            below = jnp.where(sub > t, l, 0.0)
            a_row, b_row = a_near[t : t + 1, :] * r, b_near[t : t + 1, :] * r
            a_near = jnp.where(sub == t, spread(a_row, 8), a_near - below * spread(a_row, 8))
            b_near = jnp.where(sub == t, spread(b_row, 8), b_near - below * spread(b_row, 8))
            link = {}
            for u in range(t + 1, 8):
                link[u] = l[u : u + 1, :]
                near[u] = near[u] - l * spread(link[u], 8)
            scales.append(r)
            links.append(link)
        b_ref[j : j + 8, :] = b_near
        if far:
            for t in range(8):
                l = cols[t] * spread(scales[t], far)
                for u in range(t + 1, 8):
                    cols[u] = cols[u] - l * spread(links[t][u], far)
                a_far = a_far - l * spread(a_near[t : t + 1, :], far)
                b_far = b_far - l * spread(b_near[t : t + 1, :], far)
            a_ref[j + 8 :, :] = a_far
            b_ref[j + 8 :, :] = b_far


def corner_inverse(s_top, work, a_blk, b_blk, inverse):
    eye = lax.broadcasted_iota(jnp.int32, (STEP, STEP), 0) == lax.broadcasted_iota(
        jnp.int32, (STEP, STEP), 1
    )
    eye = jnp.where(eye, 1.0, 0.0)
    count = PANEL // STEP
    for k in range(count):
        work[k, :, :PANEL] = s_top[k * STEP : (k + 1) * STEP, :]
        work[k, :, PANEL:] = jnp.zeros((STEP, PANEL), F32)
        work[k, :, PANEL + k * STEP : PANEL + (k + 1) * STEP] = eye
    lane = lax.broadcasted_iota(jnp.int32, (STEP, PANEL), 1)

    def step(k, carry):
        a_blk[...] = work[k, :, pl.ds(pl.multiple_of(k * STEP, STEP), STEP)]
        b_blk[...] = eye
        factor_inverse(a_blk, b_blk)
        rows = dot(b_blk[...], work[k], 1, 0, HIGHEST)
        work[k] = rows
        ahead = jnp.where(lane >= (k + 1) * STEP, rows[:, :PANEL], 0.0).T
        for i in range(1, count):
            work[i] = work[i] - dot(ahead[i * STEP : (i + 1) * STEP], rows, 1, 0, HIGHEST)
        return carry

    lax.fori_loop(0, count, step, 0)
    for k in range(count):
        inverse[k * STEP : (k + 1) * STEP, :] = work[k, :, PANEL:]


def coupling_of(s_rows, inv, special, step):
    inverse = inv[...]
    factor = dot(s_rows, inverse, 1, 1, HIGHEST)
    coupling = dot(factor, inverse, 1, 0, HIGHEST)
    at = pl.multiple_of(lax.rem(step, 2) * TALL, TALL)
    shape = (TALL, PANEL)
    eye = at + lax.broadcasted_iota(jnp.int32, shape, 0) == lax.broadcasted_iota(jnp.int32, shape, 1)
    top = jnp.where(eye, 1.0, 0.0) - inv[pl.ds(at, TALL), :]
    return factor, jnp.where(special, top, coupling)


def final_kernel(place, row_owner, col_owner, tiles, update, out):
    slot = pl.program_id(0)
    low = lower_half((FINE, 2 * BLOCK))
    owners = [col_owner[place[1] * 16 + j] * 2 for j in range(16)]
    for i in range(16):
        p = row_owner[place[0] * 32 + slot * 16 + i]
        for j in range(0, 16, 2):
            one = tiles[p // 2, owners[j] + p % 2]
            two = tiles[p // 2, owners[j + 1] + p % 2]
            if j < 8:
                both = jnp.where(low, one, pltpu.roll(two, BLOCK, 1))
            else:
                both = jnp.where(low, pltpu.roll(one, BLOCK, 1), two)
            at = (i, 0, slice(None), pl.ds(j * BLOCK, 2 * BLOCK))
            out[at] = both - update[at]


def axis_split(r, c):
    return r // 2, r % 2, c // 8, (c // 2) % 4, c % 2


def panel_kernel(panels, stored, h_ref, row_owner, col_owner, near, update, factor,
                 zs, cs, cp, xs, work, a_blk, b_blk, inv, corner_h, s_buf, h_buf,
                 rh, rl, lh, ll, f_buf, u_buf,
                 own_sem, p1a, p1a_got, p1x, p1x_got, p1c, p1c_got, sends, gets,
                 sib_a, sib_a_got, sib_c, sib_c_got, h_sent, h_got, out_sem):
    r, c = lax.axis_index("row"), lax.axis_index("col")
    x, yl, yh, z, core = axis_split(r, c)

    def col_of(yh_, z_, core_):
        return yh_ * 8 + (z_ % 4) * 2 + core_

    def row_of(x_, yl_):
        return (x_ % 4) * 2 + yl_

    open_sends = []

    def send(src, dst, ss, rs, to):
        copy = pltpu.make_async_remote_copy(
            src_ref=src, dst_ref=dst, send_sem=ss, recv_sem=rs, device_id=to,
            device_id_type=pl.DeviceIdType.MESH,
        )
        copy.start()
        open_sends.append(copy)

    def arrived(ref, sem):
        pltpu.make_async_copy(ref, ref, sem).wait()

    own = [
        pltpu.make_async_copy(stored.at[pl.ds(2 * r, 2)], zs.at[c, r], own_sem.at[0]),
        pltpu.make_async_copy(stored.at[c], xs.at[r, c], own_sem.at[1]),
        pltpu.make_async_copy(stored.at[0], cp.at[core, r], own_sem.at[2]),
    ]
    for copy in own:
        copy.start()
    for d in range(1, 8):
        to = (r + d) % 8
        send(panels.at[pl.ds(2 * to, 2)], zs.at[c, r], p1a.at[d], p1a_got.at[d], (to, c))
    for d in range(1, 16):
        to = (c + d) % 16
        send(panels.at[to], xs.at[r, c], p1x.at[d], p1x_got.at[d], (r, to))
    for d in range(1, 8):
        send(panels.at[0], cp.at[core, r], p1c.at[d], p1c_got.at[d], ((r + d) % 8, c))

    def h_tile(i, j):
        rows = pl.ds(pl.multiple_of(i * 128, 128), 128)
        return h_ref.at[rows, pl.ds(pl.multiple_of(j * 128, 128), 128)]

    def send_tile(n, carry):
        i, j = (r + n % 8) % 8, (c + n // 8) % 16
        pltpu.make_async_remote_copy(
            src_ref=h_tile(i, j), dst_ref=near.at[r * 16 + c], send_sem=h_sent, recv_sem=h_got,
            device_id=(i, j), device_id_type=pl.DeviceIdType.MESH,
        ).start()
        return carry

    lax.fori_loop(1, EARLY, send_tile, 0)

    zp, zm = (r, col_of(yh, z + 1, core)), (r, col_of(yh, z + 3, core))
    yp, sib = (r, col_of(1 - yh, z, core)), (r, col_of(yh, z, 1 - core))
    xp, xm, lp = (row_of(x + 1, yl), c), (row_of(x + 3, yl), c), (row_of(x, 1 - yl), c)

    def ring(ref, base, index, side, ahead, behind):
        half = ref.shape[1] // 2
        first = lambda k: ref.at[k, pl.ds(0, half)]
        second = lambda k: ref.at[k, pl.ds(half, half)]

        def out(piece, i, to):
            send(piece, piece, sends.at[base + i], gets.at[base + i], to)

        def start():
            mine = index(0, 0)
            out(ref.at[mine], 0, side)
            out(ref.at[mine], 1, ahead)
            out(ref.at[mine], 2, behind)

        def onward(plane):
            i = 1 + 4 * plane
            arrived(ref.at[index(plane, 3)], gets.at[base + i])
            out(first(index(plane, 3)), i + 2, ahead)
            arrived(ref.at[index(plane, 1)], gets.at[base + i + 1])
            out(second(index(plane, 1)), i + 3, behind)

        def beside():
            other = index(1, 0)
            arrived(ref.at[other], gets.at[base])
            out(ref.at[other], 5, ahead)
            out(ref.at[other], 6, behind)

        def last(plane):
            i = 3 + 4 * plane
            arrived(first(index(plane, 2)), gets.at[base + i])
            arrived(second(index(plane, 2)), gets.at[base + i + 1])

        return start, onward, beside, last

    def col_index(plane, d):
        return col_of(yh if plane == 0 else 1 - yh, z + d, core)

    def row_index(plane, d):
        return row_of(x + d, yl if plane == 0 else 1 - yl)

    start_a, onward_a, beside_a, last_a = ring(zs, 0, col_index, yp, zp, zm)
    start_x, onward_x, beside_x, last_x = ring(xs, 9, row_index, lp, xp, xm)
    start_c, onward_c, beside_c, last_c = ring(cs, 18, col_index, yp, zp, zm)
    shares = [(0, 0), (0, 3), (0, 1), (1, 0), (1, 3), (1, 1), (0, 2), (1, 2)]

    def share(ref, ss, rs, i):
        piece = ref.at[col_index(*shares[i])]
        send(piece, piece, ss.at[i], rs.at[i], sib)

    def shared(ref, rs, i):
        plane, d = shares[i]
        arrived(ref.at[col_of(yh if plane == 0 else 1 - yh, z + d, 1 - core)], rs.at[i])

    own[0].wait()
    for d in range(1, 8):
        arrived(zs.at[c, (r + 8 - d) % 8], p1a_got.at[d])
    start_a()
    own[1].wait()
    for d in range(1, 16):
        arrived(xs.at[r, (c + 16 - d) % 16], p1x_got.at[d])
    start_x()
    own[2].wait()
    for d in range(1, 8):
        arrived(cp.at[core, (r + 8 - d) % 8], p1c_got.at[d])
    send(cp.at[core], cp.at[core], p1c.at[0], p1c_got.at[0], sib)
    arrived(cp.at[1 - core], p1c_got.at[0])
    for i in range(4):
        p = row_owner[4 * core + i]
        cs[c, i] = cp[p % 2, p // 2]
    share(zs, sib_a, sib_a_got, 0)
    start_c()
    share(cs, sib_c, sib_c_got, 0)
    onward_x(0)
    onward_a(0)
    beside_x()
    beside_a()
    onward_c(0)
    beside_c()
    for i in range(1, 4):
        share(zs, sib_a, sib_a_got, i)
        share(cs, sib_c, sib_c_got, i)
    onward_x(1)
    onward_a(1)
    onward_c(1)
    lax.fori_loop(EARLY, 128, send_tile, 0)
    kept = pltpu.make_async_copy(h_tile(r, c), near.at[r * 16 + c], h_got)
    kept.start()
    for i in range(4, 6):
        share(cs, sib_c, sib_c_got, i)
        share(zs, sib_a, sib_a_got, i)
    last_a(0)
    share(zs, sib_a, sib_a_got, 6)
    last_c(0)
    share(cs, sib_c, sib_c_got, 6)
    last_c(1)
    share(cs, sib_c, sib_c_got, 7)
    for i in range(8):
        shared(cs, sib_c_got, i)

    fetch_panel(
        lambda i, p, q: cs[2 * q + i // 4, i % 4],
        PANEL // BLOCK, 0, row_owner, col_owner, s_buf, corner_h,
    )
    corner_inverse(s_buf, work, a_blk, b_blk, inv)
    last_a(1)
    share(zs, sib_a, sib_a_got, 7)
    for plane in range(2):
        last_x(plane)

    def strip_step(t, carry):
        fetch_panel(
            lambda i, p, q: xs[p // 2, 2 * q + p % 2],
            TALL // BLOCK, c * 16 + t * 4, row_owner, col_owner, s_buf, h_buf,
        )
        special = jnp.logical_and(c == 0, t < 2)
        _, coupling = coupling_of(s_buf[:TALL, :], inv, special, t)
        rest = h_buf[...] - dot(coupling, corner_h[...], 1, 0, HIGHEST)
        at = pl.ds(pl.multiple_of(t * TALL, TALL), TALL)
        rh[at, :PANEL], rl[at, :PANEL] = halves(rest)
        rh[at, PANEL:], rl[at, PANEL:] = halves(coupling)
        return carry

    lax.fori_loop(0, rh.shape[0] // TALL, strip_step, 0)
    for i in range(8):
        shared(zs, sib_a_got, i)

    def rows_of(t):
        return pl.ds(pl.multiple_of(t * TALL, TALL), TALL)

    def band_step(t, carry):
        slot = t // 4
        fetch_panel(
            lambda i, p, q: zs[2 * q + p % 2, p // 2, slot],
            TALL // BLOCK, r * 32 + t * 4, row_owner, col_owner, s_buf, h_buf,
        )
        special = jnp.logical_and(r == 0, t < 2)
        panel, coupling = coupling_of(s_buf[:TALL, :], inv, special, t)
        f_buf[rows_of(t), :] = panel
        lh[:, :PANEL], ll[:, :PANEL] = halves(coupling)
        lh[:, PANEL:], ll[:, PANEL:] = halves(h_buf[...])
        total = dot(lh[...], rh[...], 1, 1)
        total = total + dot(lh[...], rl[...], 1, 1)
        u_buf[rows_of(t), :] = total + dot(ll[...], rh[...], 1, 1)
        pltpu.make_async_copy(u_buf.at[rows_of(t)], update.at[rows_of(t)], out_sem.at[0, t]).start()
        pltpu.make_async_copy(f_buf.at[rows_of(t)], factor.at[rows_of(t)], out_sem.at[1, t]).start()
        return carry

    steps = u_buf.shape[0] // TALL
    lax.fori_loop(0, steps, band_step, 0)
    for t in range(steps):
        pltpu.make_async_copy(u_buf.at[rows_of(t)], update.at[rows_of(t)], out_sem.at[0, t]).wait()
        pltpu.make_async_copy(f_buf.at[rows_of(t)], factor.at[rows_of(t)], out_sem.at[1, t]).wait()
    arrived(near, h_got)
    arrived(near.at[pl.ds(0, 127)], h_sent)
    for copy in open_sends:
        copy.wait_send()


SMEM = pl.BlockSpec(memory_space=pltpu.SMEM)


def shape_of(shape, dtype=F32):
    return jax.ShapeDtypeStruct(shape, dtype)


def per_device(h_old, s_old, row_owner, col_owner):
    rows_n = lax.axis_size("row")
    cols_n = lax.axis_size("col")
    row_id = lax.axis_index("row")
    col_id = lax.axis_index("col")
    place = jnp.stack([row_id, col_id]).astype(jnp.int32)
    local_h = h_old[0, 0]
    local_s = s_old[0, 0]
    band = ORDER // rows_n
    strip = ORDER // cols_n
    panels = jnp.concatenate([local_s, local_h[:, :BLOCK]], axis=1).reshape(16, BLOCK, 128)
    any_space = pl.BlockSpec(memory_space=pl.ANY)
    dma = pltpu.SemaphoreType.DMA
    vmem = pltpu.VMEM
    near, update, factor = pl.pallas_call(
        panel_kernel,
        out_shape=(shape_of((128, 128, 128)), shape_of((band, strip)), shape_of((band, PANEL))),
        in_specs=[pl.BlockSpec(memory_space=pltpu.VMEM), any_space, any_space, SMEM, SMEM],
        out_specs=(any_space,) * 3,
        scratch_shapes=[
            vmem((16, 8, 2, BLOCK, 128), F32),
            vmem((16, 4, BLOCK, 128), F32),
            vmem((2, 8, BLOCK, 128), F32),
            vmem((8, 16, BLOCK, 128), F32),
            vmem((PANEL // STEP, STEP, 2 * PANEL), F32),
            vmem((STEP, STEP), F32),
            vmem((STEP, STEP), F32),
            vmem((PANEL, PANEL), F32),
            vmem((PANEL, PANEL), F32),
            vmem((PANEL, PANEL), F32),
            vmem((TALL, PANEL), F32),
            vmem((strip, 2 * PANEL), BF16),
            vmem((strip, 2 * PANEL), BF16),
            vmem((TALL, 2 * PANEL), BF16),
            vmem((TALL, 2 * PANEL), BF16),
            vmem((band, PANEL), F32),
            vmem((band, strip), F32),
            dma((3,)), dma((8,)), dma((8,)), dma((16,)), dma((16,)), dma((8,)), dma((8,)),
            dma((27,)), dma((27,)), dma((8,)), dma((8,)), dma((8,)), dma((8,)), dma, dma,
            dma((2, band // TALL)),
        ],
        compiler_params=pltpu.CompilerParams(has_side_effects=True, vmem_limit_bytes=60 * 2**20),
        cost_estimate=pl.CostEstimate(flops=4 * 10**10, bytes_accessed=64 * 2**20, transcendentals=0),
        name="panel",
    )(panels, panels, local_h, row_owner, col_owner)
    h_tiles = near.reshape(rows_n, cols_n, 128, 128)

    fine = pl.BlockSpec((16, 1, FINE, strip), lambda s, u: (s, u, 0, 0))
    h_block = pl.pallas_call(
        final_kernel,
        grid=(2, BLOCK // FINE),
        out_shape=shape_of((band // BLOCK, BLOCK // FINE, FINE, strip)),
        in_specs=[
            SMEM, SMEM, SMEM,
            pl.BlockSpec((rows_n, cols_n, FINE, 128), lambda s, u: (0, 0, s * (BLOCK // FINE) + u, 0)),
            fine,
        ],
        out_specs=fine,
        compiler_params=pltpu.CompilerParams(vmem_limit_bytes=60 * 2**20),
        cost_estimate=pl.CostEstimate(flops=2**22, bytes_accessed=24 * 2**20, transcendentals=0),
        name="final",
    )(place, row_owner, col_owner, h_tiles, update.reshape(band // BLOCK, BLOCK // FINE, FINE, strip))
    return h_block.reshape(band, strip), factor


def solution(mesh):
    in_specs = (P("row", "col", None, None), P("row", "col", None, None), P(), P())
    out_specs = (P("row", "col"), P("row", None))
    return jax.shard_map(
        per_device, mesh=mesh, in_specs=in_specs, out_specs=out_specs, check_vma=False
    )
```

time: 394 us -> 235 us (0.60)
  waiting for transfers between devices: 210 us -> 0 us
  Pallas kernels: 81.9 us -> 222 us
  blocking collectives: 63.2 us -> 0 us
  between operations: 13.8 us -> 0.65 us
  starting transfers between devices: 9.08 us -> 0 us
  local copies, waits for them, and re-layouts: 14.5 us -> 6.86 us
    all_gather x3 -> x0, waiting for transfers between devices: 210 us -> none  [the longest x1 142 us: per_device(): strip_tiles = lax.all_gather(strip_tiles, 'row', axis=0)]
    pallas_call x4 -> x2, Pallas kernels: 81.9 us -> 222 us  [the longest x1 210 us: per_device(): pl.pallas_call(panel_kernel, out_shape=(shape_of((128, 128, 128)), shape_...]
    all_to_all x2 -> x0, blocking collectives: 38.2 us -> none  [the longest x1 27.5 us: per_device(): lax.all_to_all(panels.reshape(cols_n, BLOCK, 128), 'col', 0, 0, tiled=True)]
    all_gather x1 -> x0, blocking collectives: 25 us -> none  [per_device(): top = lax.all_gather(panels[:BLOCK], 'row', axis=0)]
    all_to_all x1 -> x0, starting transfers between devices: 8.95 us -> none  [per_device(): lax.all_to_all(outgoing.reshape(rows_n * cols_n, 128, 128), ('row', 'col'...]
    transpose x2 -> x0, local copies, waits for them, and re-layouts: 6.44 us -> none  [per_device(): outgoing = local_h.reshape(rows_n, 128, cols_n, 128).transpose(0, 2, 1, 3)]
  transfers between devices with their start and end apart: 4 -> 0, of which waited for: 3 -> 0; matrix products, arithmetic and copies ran while one was open for 3% -> 0% of each run, Pallas kernels for 15% -> 0%
where the time goes in v5:
time: 235 us; the launch traced here: 231 us
  Pallas kernels  222 us (94%)
  local copies, waits for them, and re-layouts  6.86 us (3%)
    pallas_call x1, Pallas kernels, per_device(): pl.pallas_call(panel_kernel, out_shape=(shape_of((128, 128, 128)), shape_...  210 us
    pallas_call x1, Pallas kernels, per_device(): pl.pallas_call(final_kernel, grid=(2, BLOCK // FINE), out_shape=shape_of(...  12.2 us
    unnamed x2, local copies, waits for them, and re-layouts  5.78 us

profile of v5, /device:TPU:1, one launch (start us, length us, event | category | flops | bytes accessed | tf_op | source)
XLA Modules:
  0.0 231.1 jit_solution(5422131042890020026)
XLA Ops:
  0.6 0.6 pad_add_fusion.place
  1.2 1.1 slice.4
  2.3 1.1 copy.6
  3.5 1.0 pad_maximum_fusion.panels.stored
  4.5 209.8 %panel.1 = (f32[128,128,128]{2,1,0:T(8,128)}, f32[2048,1024]{1,0:T(8,128)}, f32[2048,512]{1,0:T(8,128)}) custom-call(f32[16,64,128]{2,1,0:T(8,128)} %pad_maximum_fusion.panels.stored, f32[16,64,128]{2,1,0:T(8,128)} %pad_maximum_fusion.panels.stored, f32[1024,2048]{1,0:T(8,128)} %bitcast.14, s32[256]{0:T(256)} %row_owner.3, s32[256]{0:T(256)} %col_owner.3), custom_call_target="tpu_custom_call" | custom-call | flops 40000000000 | bytes 67108864 | tf_op jit(solution)/shard_map/panel/pallas_call | solution.py:386
  214.3 12.2 %final.1 = f32[32,4,16,1024]{3,2,1,0:T(8,128)} custom-call(s32[2]{0:T(128)} %pad_add_fusion.place, s32[256]{0:T(256)} %row_owner.3, s32[256]{0:T(256)} %col_owner.3, f32[8,16,128,128]{3,2,1,0:T(8,128)} %bitcast.9, f32[32,4,16,1024]{3,2,1,0:T(8,128)} %bitcast.10), custom_call_target="tpu_custom_call" | custom-call | flops 4194304 | bytes 25165824 | tf_op jit(solution)/shard_map/final/pallas_call | solution.py:420
  226.5 4.6 %copy.8 = f32[2048,512]{1,0:T(8,128)} copy(f32[2048,512]{1,0:T(8,128)} %get-tuple-element.11) | data formatting | bytes 8388608

commit v6 on v5

--- a/solution.py
+++ b/solution.py
@@ -11,7 +11,7 @@
 STEP = 128
 FINE = 16
 TALL = 256
-EARLY = 16
+EARLY = 1
 HIGHEST = lax.Precision.HIGHEST
 BF16 = jnp.bfloat16
 F32 = jnp.float32
@@ -191,7 +191,9 @@
         return h_ref.at[rows, pl.ds(pl.multiple_of(j * 128, 128), 128)]
 
     def send_tile(n, carry):
-        i, j = (r + n % 8) % 8, (c + n // 8) % 16
+        m = n * (37 + 54 * core) % 128
+        i = row_of(x + m % 4, (yl + m // 4) % 2)
+        j = col_of((2 * yh + yl + m // 4) // 2 % 2, z + m // 16, (core + m // 64) % 2)
         pltpu.make_async_remote_copy(
             src_ref=h_tile(i, j), dst_ref=near.at[r * 16 + c], send_sem=h_sent, recv_sem=h_got,
             device_id=(i, j), device_id_type=pl.DeviceIdType.MESH,
@@ -288,9 +290,6 @@
     onward_x(1)
     onward_a(1)
     onward_c(1)
-    lax.fori_loop(EARLY, 128, send_tile, 0)
-    kept = pltpu.make_async_copy(h_tile(r, c), near.at[r * 16 + c], h_got)
-    kept.start()
     for i in range(4, 6):
         share(cs, sib_c, sib_c_got, i)
         share(zs, sib_a, sib_a_got, i)
@@ -303,15 +302,20 @@
     for i in range(8):
         shared(cs, sib_c_got, i)
 
+    last_a(1)
+    share(zs, sib_a, sib_a_got, 7)
+    for plane in range(2):
+        last_x(plane)
+    for i in range(8):
+        shared(zs, sib_a_got, i)
+    lax.fori_loop(EARLY, 128, send_tile, 0)
+    kept = pltpu.make_async_copy(h_tile(r, c), near.at[r * 16 + c], h_got)
+    kept.start()
     fetch_panel(
         lambda i, p, q: cs[2 * q + i // 4, i % 4],
         PANEL // BLOCK, 0, row_owner, col_owner, s_buf, corner_h,
     )
     corner_inverse(s_buf, work, a_blk, b_blk, inv)
-    last_a(1)
-    share(zs, sib_a, sib_a_got, 7)
-    for plane in range(2):
-        last_x(plane)
 
     def strip_step(t, carry):
         fetch_panel(
@@ -327,8 +331,6 @@
         return carry
 
     lax.fori_loop(0, rh.shape[0] // TALL, strip_step, 0)
-    for i in range(8):
-        shared(zs, sib_a_got, i)
 
     def rows_of(t):
         return pl.ds(pl.multiple_of(t * TALL, TALL), TALL)

time: 235 us -> 198 us (0.84); the launches traced: 231 us -> 198 us
  Pallas kernels: 222 us -> 189 us
    pallas_call x1, Pallas kernels: 210 us -> 176 us  [per_device(): pl.pallas_call(panel_kernel, out_shape=(shape_of((128, 128, 128)), shape_...]
where the time goes in v6:
time: 198 us
  Pallas kernels  189 us (95%)
  local copies, waits for them, and re-layouts  6.86 us (3%)
    pallas_call x1, Pallas kernels, per_device(): pl.pallas_call(panel_kernel, out_shape=(shape_of((128, 128, 128)), shape_...  176 us
    pallas_call x1, Pallas kernels, per_device(): pl.pallas_call(final_kernel, grid=(2, BLOCK // FINE), out_shape=shape_of(...  12.2 us
    unnamed x2, local copies, waits for them, and re-layouts  5.78 us

profile of v6, /device:TPU:1, one launch (start us, length us, event | category | flops | bytes accessed | tf_op | source)
XLA Modules:
  0.0 197.6 jit_solution(10981065206345762623)
XLA Ops:
  0.6 0.6 pad_add_fusion.place
  1.2 1.1 slice.4
  2.3 1.1 copy.6
  3.5 1.0 pad_maximum_fusion.panels.stored
  4.5 176.3 %panel.1 = (f32[128,128,128]{2,1,0:T(8,128)}, f32[2048,1024]{1,0:T(8,128)}, f32[2048,512]{1,0:T(8,128)}) custom-call(f32[16,64,128]{2,1,0:T(8,128)} %pad_maximum_fusion.panels.stored, f32[16,64,128]{2,1,0:T(8,128)} %pad_maximum_fusion.panels.stored, f32[1024,2048]{1,0:T(8,128)} %bitcast.14, s32[256]{0:T(256)} %row_owner.3, s32[256]{0:T(256)} %col_owner.3), custom_call_target="tpu_custom_call" | custom-call | flops 40000000000 | bytes 67108864 | tf_op jit(solution)/shard_map/panel/pallas_call | solution.py:388
  180.7 12.2 %final.1 = f32[32,4,16,1024]{3,2,1,0:T(8,128)} custom-call(s32[2]{0:T(128)} %pad_add_fusion.place, s32[256]{0:T(256)} %row_owner.3, s32[256]{0:T(256)} %col_owner.3, f32[8,16,128,128]{3,2,1,0:T(8,128)} %bitcast.9, f32[32,4,16,1024]{3,2,1,0:T(8,128)} %bitcast.10), custom_call_target="tpu_custom_call" | custom-call | flops 4194304 | bytes 25165824 | tf_op jit(solution)/shard_map/final/pallas_call | solution.py:422
  193.0 4.6 %copy.8 = f32[2048,512]{1,0:T(8,128)} copy(f32[2048,512]{1,0:T(8,128)} %get-tuple-element.11) | data formatting | bytes 8388608

commit v7 on v6

--- a/solution.py
+++ b/solution.py
@@ -9,7 +9,7 @@
 PANEL = 512
 BLOCK = 64
 STEP = 128
-FINE = 16
+FINE = 32
 TALL = 256
 EARLY = 1
 HIGHEST = lax.Precision.HIGHEST
@@ -278,17 +278,17 @@
     share(zs, sib_a, sib_a_got, 0)
     start_c()
     share(cs, sib_c, sib_c_got, 0)
+    onward_a(0)
     onward_x(0)
-    onward_a(0)
+    beside_a()
     beside_x()
-    beside_a()
     onward_c(0)
     beside_c()
     for i in range(1, 4):
         share(zs, sib_a, sib_a_got, i)
         share(cs, sib_c, sib_c_got, i)
+    onward_a(1)
     onward_x(1)
-    onward_a(1)
     onward_c(1)
     for i in range(4, 6):
         share(cs, sib_c, sib_c_got, i)
@@ -299,18 +299,18 @@
     share(cs, sib_c, sib_c_got, 6)
     last_c(1)
     share(cs, sib_c, sib_c_got, 7)
-    for i in range(8):
-        shared(cs, sib_c_got, i)
-
     last_a(1)
     share(zs, sib_a, sib_a_got, 7)
+    lax.fori_loop(EARLY, 128, send_tile, 0)
+    kept = pltpu.make_async_copy(h_tile(r, c), near.at[r * 16 + c], h_got)
+    kept.start()
     for plane in range(2):
         last_x(plane)
     for i in range(8):
+        shared(cs, sib_c_got, i)
+    for i in range(8):
         shared(zs, sib_a_got, i)
-    lax.fori_loop(EARLY, 128, send_tile, 0)
-    kept = pltpu.make_async_copy(h_tile(r, c), near.at[r * 16 + c], h_got)
-    kept.start()
+
     fetch_panel(
         lambda i, p, q: cs[2 * q + i // 4, i % 4],
         PANEL // BLOCK, 0, row_owner, col_owner, s_buf, corner_h,

time: 198 us -> 191 us (0.965); the launches traced: 198 us -> 189 us
  Pallas kernels: 189 us -> 179 us
    pallas_call x1, Pallas kernels: 176 us -> 170 us  [per_device(): pl.pallas_call(panel_kernel, out_shape=(shape_of((128, 128, 128)), shape_...]
    pallas_call x1, Pallas kernels: 12.2 us -> 9.86 us  [per_device(): pl.pallas_call(final_kernel, grid=(2, BLOCK // FINE), out_shape=shape_of(...]
where the time goes in v7:
time: 191 us; the launch traced here: 189 us
  Pallas kernels  179 us (94%)
  local copies, waits for them, and re-layouts  6.86 us (4%)
    pallas_call x1, Pallas kernels, per_device(): pl.pallas_call(panel_kernel, out_shape=(shape_of((128, 128, 128)), shape_...  170 us
    pallas_call x1, Pallas kernels, per_device(): pl.pallas_call(final_kernel, grid=(2, BLOCK // FINE), out_shape=shape_of(...  9.86 us
    unnamed x2, local copies, waits for them, and re-layouts  5.78 us

profile of v7, /device:TPU:1, one launch (start us, length us, event | category | flops | bytes accessed | tf_op | source)
XLA Modules:
  0.0 188.5 jit_solution(17677074716880824315)
XLA Ops:
  0.6 0.6 pad_add_fusion.place
  1.2 1.1 slice.4
  2.3 1.1 copy.6
  3.5 1.0 pad_maximum_fusion.panels.stored
  4.5 169.6 %panel.1 = (f32[128,128,128]{2,1,0:T(8,128)}, f32[2048,1024]{1,0:T(8,128)}, f32[2048,512]{1,0:T(8,128)}) custom-call(f32[16,64,128]{2,1,0:T(8,128)} %pad_maximum_fusion.panels.stored, f32[16,64,128]{2,1,0:T(8,128)} %pad_maximum_fusion.panels.stored, f32[1024,2048]{1,0:T(8,128)} %bitcast.14, s32[256]{0:T(256)} %row_owner.3, s32[256]{0:T(256)} %col_owner.3), custom_call_target="tpu_custom_call" | custom-call | flops 40000000000 | bytes 67108864 | tf_op jit(solution)/shard_map/panel/pallas_call | solution.py:388
  174.0 9.9 %final.1 = f32[32,2,32,1024]{3,2,1,0:T(8,128)} custom-call(s32[2]{0:T(128)} %pad_add_fusion.place, s32[256]{0:T(256)} %row_owner.3, s32[256]{0:T(256)} %col_owner.3, f32[8,16,128,128]{3,2,1,0:T(8,128)} %bitcast.9, f32[32,2,32,1024]{3,2,1,0:T(8,128)} %bitcast.10), custom_call_target="tpu_custom_call" | custom-call | flops 4194304 | bytes 25165824 | tf_op jit(solution)/shard_map/final/pallas_call | solution.py:422
  183.9 4.6 %copy.8 = f32[2048,512]{1,0:T(8,128)} copy(f32[2048,512]{1,0:T(8,128)} %get-tuple-element.11) | data formatting | bytes 8388608

commit v8 on v7

--- a/solution.py
+++ b/solution.py
@@ -191,7 +191,7 @@
         return h_ref.at[rows, pl.ds(pl.multiple_of(j * 128, 128), 128)]
 
     def send_tile(n, carry):
-        m = n * (37 + 54 * core) % 128
+        m = n * (45 + 38 * core) % 128
         i = row_of(x + m % 4, (yl + m // 4) % 2)
         j = col_of((2 * yh + yl + m // 4) // 2 % 2, z + m // 16, (core + m // 64) % 2)
         pltpu.make_async_remote_copy(

time: 191 us -> 191 us (level)
  the two profiles are of different devices: /device:TPU:1 before, /device:TPU:26 now
where the time goes in v8:
time: 191 us
  Pallas kernels  182 us (95%)
  local copies, waits for them, and re-layouts  6.86 us (4%)
    pallas_call x1, Pallas kernels, per_device(): pl.pallas_call(panel_kernel, out_shape=(shape_of((128, 128, 128)), shape_...  172 us
    pallas_call x1, Pallas kernels, per_device(): pl.pallas_call(final_kernel, grid=(2, BLOCK // FINE), out_shape=shape_of(...  9.86 us
    unnamed x2, local copies, waits for them, and re-layouts  5.78 us

profile of v8, /device:TPU:26, one launch (start us, length us, event | category | flops | bytes accessed | tf_op | source)
XLA Modules:
  0.0 190.8 jit_solution(4478677974068212713)
XLA Ops:
  0.6 0.6 pad_add_fusion.place
  1.2 1.1 slice.4
  2.3 1.1 copy.6
  3.5 1.0 pad_maximum_fusion.panels.stored
  4.5 171.8 %panel.1 = (f32[128,128,128]{2,1,0:T(8,128)}, f32[2048,1024]{1,0:T(8,128)}, f32[2048,512]{1,0:T(8,128)}) custom-call(f32[16,64,128]{2,1,0:T(8,128)} %pad_maximum_fusion.panels.stored, f32[16,64,128]{2,1,0:T(8,128)} %pad_maximum_fusion.panels.stored, f32[1024,2048]{1,0:T(8,128)} %bitcast.14, s32[256]{0:T(256)} %row_owner.3, s32[256]{0:T(256)} %col_owner.3), custom_call_target="tpu_custom_call" | custom-call | flops 40000000000 | bytes 67108864 | tf_op jit(solution)/shard_map/panel/pallas_call | solution.py:388
  176.3 9.9 %final.1 = f32[32,2,32,1024]{3,2,1,0:T(8,128)} custom-call(s32[2]{0:T(128)} %pad_add_fusion.place, s32[256]{0:T(256)} %row_owner.3, s32[256]{0:T(256)} %col_owner.3, f32[8,16,128,128]{3,2,1,0:T(8,128)} %bitcast.9, f32[32,2,32,1024]{3,2,1,0:T(8,128)} %bitcast.10), custom_call_target="tpu_custom_call" | custom-call | flops 4194304 | bytes 25165824 | tf_op jit(solution)/shard_map/final/pallas_call | solution.py:422
  186.1 4.6 %copy.8 = f32[2048,512]{1,0:T(8,128)} copy(f32[2048,512]{1,0:T(8,128)} %get-tuple-element.11) | data formatting | bytes 8388608
